TPU v7x, 256 devices: a whole 4x4x8 slice. The times are simulated.
256 devices in a mesh: panel: 4 (over x_hi, core), tile: 64 (over y, x_lo, z).
Axes of the slice: x: 4 (x_hi: 2, x_lo: 2; x = x_hi * 2 + x_lo), y: 4, z: 8, core: 2. Of those that a mesh axis runs over, the one named last changes fastest.
Arguments:
- residual: float32 [4, 64, 128, 8, 128], P('panel', 'tile'), may hold values from -6 to 6
- inverse: bfloat16 [4, 64, 16, 576, 576], P('panel', 'tile'), may hold values from -1 to 2
- blend_weight: float32 [576], replicated, may hold values from 0.1 to 1.9
- seam_table: int32 [4, 4, 3], replicated, may hold values from -1 to 3, as said below
Outputs:
- correction: float32 [4, 64, 128, 8, 128], P('panel', 'tile')
Inputs may be any that keep to these rules, and one draw needn't show every extreme that they name: seam_table[p, e] holds the neighbour panel across edge e of panel p (or -1), a rotation r and a reversal v. Every panel has neighbours across exactly two opposite edges (0 and 2, or 1 and 3) and the entries -1, 0, 0 on the other two; the panels form one closed cycle and each panel's two neighbours differ. If edge e of p faces panel q, then edge c = (e + 2 + r) mod 4 of q faces p with rotation (-r) mod 4 and the same reversal v. At least one seam joins edge 0 of a panel to edge 0 of another, with rotation 2 and reversal 1.
All inputs are finite; a program needn't handle non-finite values.
Results may differ from a plain program's by a relative error of at most 0.0029.
Values may be sent and summed in bfloat16 or wider, within the bound.
A program may use at most 128 MiB of HBM per device.

v0:
```python
import jax
import jax.numpy as jnp
from jax import lax
from jax.sharding import PartitionSpec as P

PANELS = 4
TILE_ROWS = 2
SUB = 8
INTERSECTION = 8


def passed_along(block, axis, distance):
    devices = range(lax.axis_size(axis))
    route = [(i - distance, i) for i in devices if i - distance in devices]
    return lax.ppermute(block, axis, route)


def in_blocks(value, dim, peers):
    before, after = (value.shape[:dim], value.shape[dim + 1 :])
    return jnp.moveaxis(value.reshape(*before, peers, -1, *after), dim, 0)


def summed_on_arrival(value, axis, dim):
    peers = lax.axis_size(axis)
    pieces = lax.all_to_all(in_blocks(value, dim, peers), axis, 0, 0, tiled=True)
    return jnp.sum(pieces.astype(jnp.float32), axis=0)


def rows_for(lines, peers):
    spare = -len(lines) % peers
    return jnp.pad(lines, [(0, spare)] + [(0, 0)] * (lines.ndim - 1))


def copy_for_each(value, axis):
    peers = lax.axis_size(axis)
    return lax.all_to_all(
        jnp.broadcast_to(value[None], (peers, *value.shape)), axis, 0, 0, tiled=True
    )


def laid_out(pieces, dim):
    shape = list(pieces.shape[1:])
    shape[dim] *= pieces.shape[0]
    return jnp.moveaxis(pieces, 0, dim).reshape(shape)


def gather_directly(value, axis, dim):
    pieces = copy_for_each(value, axis)
    return laid_out(pieces, dim)


def sum_by_parts(value, axes):
    lines = value.reshape(-1, value.shape[-1])
    own = summed_on_arrival(rows_for(lines, lax.axis_size(axes)), axes, 0)
    whole = gather_directly(own.astype(jnp.bfloat16), axes, 0)
    return whole[: len(lines)].reshape(value.shape).astype(jnp.float32)


def neighbours_in(first_part, second_part, stride):
    from_below = passed_along(first_part, "tile", stride)
    from_above = passed_along(second_part, "tile", -stride)
    return (from_below, from_above)


def neighbours_out(first_part, second_part, stride):
    to_above = passed_along(first_part.astype(jnp.bfloat16), "tile", stride).astype(
        first_part.dtype
    )
    to_below = passed_along(second_part.astype(jnp.bfloat16), "tile", -stride).astype(
        second_part.dtype
    )
    return (to_above, to_below)


def band_index(edge_id, row_count, col_count):
    margin = INTERSECTION
    if edge_id == 0:
        return (slice(None), slice(0, margin))
    if edge_id == 1:
        return (slice(0, margin), slice(None))
    if edge_id == 2:
        return (slice(None), slice(col_count - margin, col_count))
    return (slice(row_count - margin, row_count), slice(None))


def to_band(window, edge_id):
    if edge_id == 0:
        return jnp.transpose(window[::-1], (1, 0, 2))
    if edge_id == 1:
        return window[::-1]
    if edge_id == 2:
        return jnp.transpose(window, (1, 0, 2))
    return window


def from_band(region, edge_id):
    if edge_id == 0:
        return jnp.transpose(region, (1, 0, 2))[::-1]
    if edge_id == 1:
        return region[::-1]
    if edge_id == 2:
        return jnp.transpose(region, (1, 0, 2))
    return region


def into_cells(edge_part, edge_id):
    if edge_id == 0:
        return jnp.transpose(edge_part, (1, 0, 2))
    if edge_id == 1:
        return edge_part
    if edge_id == 2:
        return jnp.transpose(edge_part[::-1], (1, 0, 2))
    return edge_part[::-1]


def placed(band, offset, live_edge, length_all):
    band = band.astype(jnp.float32)
    blank_band = jnp.zeros((band.shape[0], length_all, band.shape[2]), jnp.float32)
    filled = lax.dynamic_update_slice_in_dim(blank_band, band, offset, 1)
    return jnp.where(live_edge, filled, jnp.zeros_like(filled))


def build_buffer(bands, offsets, live_edge, panel_side, extra):
    length_all = panel_side + 2 * extra
    return jnp.stack(
        [
            (
                placed(bands[2 * slot_id], offsets[2 * slot_id], live_edge[2 * slot_id], length_all)
                + placed(
                    bands[2 * slot_id + 1],
                    offsets[2 * slot_id + 1],
                    live_edge[2 * slot_id + 1],
                    length_all,
                )
            )[:, extra : extra + panel_side]
            for slot_id in range(2)
        ]
    )


def slot_info(seam_row, slot_id):
    first_entry = seam_row[2 * slot_id]
    second_entry = seam_row[2 * slot_id + 1]
    first_live = first_entry[0] >= 0
    chosen = jnp.where(first_live, first_entry, second_entry)
    edge_id = jnp.where(first_live, 2 * slot_id, 2 * slot_id + 1)
    facing = (edge_id + 2 + chosen[1]) % 4
    return (jnp.maximum(chosen[0], 0), facing // 2, chosen[2])


def outgoing_of(totals, slot_facts):
    blank_slot = jnp.zeros_like(totals[0])
    return jnp.stack(
        [
            jnp.where(
                slot_facts[0][0] == target,
                totals[0],
                jnp.where(slot_facts[1][0] == target, totals[1], blank_slot),
            )
            for target in range(PANELS)
        ]
    )


def picked_of(arrived_all, slot_facts):
    return jnp.stack(
        [
            lax.dynamic_index_in_dim(arrived_all, slot_facts[slot_id][0], 0, keepdims=False)
            for slot_id in range(2)
        ]
    )


def cross(bands, seam_row, forward, offsets, live_edge, panel_side):
    extra = 0 if forward else INTERSECTION
    slot_facts = [slot_info(seam_row, slot_id) for slot_id in range(2)]
    buffer = build_buffer(bands, offsets, live_edge, panel_side, extra)
    if forward:
        totals = sum_by_parts(buffer.astype(jnp.bfloat16), "tile").astype(jnp.bfloat16)
        arrived_all = lax.all_to_all(
            outgoing_of(totals, slot_facts), "panel", split_axis=0, concat_axis=0, tiled=True
        )
    else:
        totals = sum_by_parts(buffer.astype(jnp.bfloat16), "tile")
        arrived_all = lax.all_to_all(
            outgoing_of(totals, slot_facts).astype(jnp.bfloat16),
            "panel",
            split_axis=0,
            concat_axis=0,
            tiled=True,
        ).astype(jnp.float32)
    arrived = picked_of(arrived_all, slot_facts)
    return [
        jnp.where(slot_facts[slot_id][2] > 0, arrived[slot_id][:, ::-1], arrived[slot_id])
        for slot_id in range(2)
    ]


def patches(padded, block_rows, block_cols):
    columns = padded.shape[-1]
    blocked = padded.reshape(block_rows + 2, SUB, block_cols + 2, SUB, columns)
    pieces = [
        blocked[row_shift : row_shift + block_rows, :, col_shift : col_shift + block_cols]
        for row_shift in range(3)
        for col_shift in range(3)
    ]
    stacked = jnp.stack(pieces).reshape(3, 3, block_rows, SUB, block_cols, SUB, columns)
    stacked = jnp.transpose(stacked, (2, 4, 0, 3, 1, 5, 6))
    return stacked.reshape(block_rows, block_cols, 9 * SUB * SUB, columns)


def intersection_add(solved, block_rows, block_cols):
    columns = solved.shape[-1]
    shaped = solved.reshape(block_rows, block_cols, 3, SUB, 3, SUB, columns)
    summed = jnp.zeros((block_rows + 2, SUB, block_cols + 2, SUB, columns), jnp.float32)
    for row_shift in range(3):
        for col_shift in range(3):
            block_part = jnp.transpose(shaped[:, :, row_shift, :, col_shift], (0, 2, 1, 3, 4))
            summed = summed.at[
                row_shift : row_shift + block_rows, :, col_shift : col_shift + block_cols
            ].add(block_part)
    return summed.reshape((block_rows + 2) * SUB, (block_cols + 2) * SUB, columns)


def local(residual, inverse, blend_weight, seam_table):
    margin = INTERSECTION
    source = residual[0, 0].astype(jnp.bfloat16)
    height, tile_width, columns = source.shape
    tile_rows = TILE_ROWS
    tile_cols = lax.axis_size("tile") // TILE_ROWS
    tile_id = lax.axis_index("tile")
    row_pos = tile_id // tile_cols
    col_pos = tile_id % tile_cols
    seam_row = lax.dynamic_index_in_dim(seam_table, lax.axis_index("panel"), 0, keepdims=False)
    panel_side = tile_width * tile_cols
    on_edge = [col_pos == 0, row_pos == 0, col_pos == tile_cols - 1, row_pos == tile_rows - 1]
    live_edge = [on_edge[edge_id] & (seam_row[edge_id, 0] >= 0) for edge_id in range(4)]
    offsets = [row_pos * height, col_pos * tile_width, row_pos * height, col_pos * tile_width]
    lengths = [height, tile_width, height, tile_width]
    left_valid = col_pos > 0
    right_valid = col_pos < tile_cols - 1
    below_rows, above_rows = neighbours_in(source[height - margin :], source[:margin], tile_cols)
    row_ext = jnp.concatenate([below_rows, source, above_rows], 0)
    left_cols, right_cols = neighbours_in(row_ext, row_ext, 1)
    left_cols = jnp.where(left_valid, left_cols, jnp.zeros_like(left_cols))
    right_cols = jnp.where(right_valid, right_cols, jnp.zeros_like(right_cols))
    extended = jnp.concatenate([left_cols, row_ext, right_cols], 1)
    own_strips = [
        jnp.transpose(source, (1, 0, 2)),
        source[:margin],
        jnp.transpose(source[:, ::-1], (1, 0, 2)),
        source[height - margin :][::-1],
    ]
    arrived = cross(own_strips, seam_row, True, offsets, live_edge, panel_side)
    rows_ext, cols_ext = (extended.shape[0], extended.shape[1])
    for edge_id in range(4):
        widened = jnp.pad(arrived[edge_id // 2], ((0, 0), (margin, margin), (0, 0)))
        window = lax.dynamic_slice_in_dim(
            widened, offsets[edge_id], lengths[edge_id] + 2 * margin, 1
        )
        where_band = band_index(edge_id, rows_ext, cols_ext)
        fresh_band = jnp.where(live_edge[edge_id], to_band(window, edge_id), extended[where_band])
        extended = extended.at[where_band].set(fresh_band)
    sub_rows, sub_cols = (height // SUB, tile_width // SUB)
    local_patches = patches(extended, sub_rows, sub_cols).reshape(
        sub_rows * sub_cols, 9 * SUB * SUB, columns
    )
    solved = jnp.einsum(
        "noi,nir->nor", inverse[0, 0], local_patches, preferred_element_type=jnp.float32
    )
    solved = solved * blend_weight[None, :, None]
    spread = intersection_add(
        solved.reshape(sub_rows, sub_cols, 9 * SUB * SUB, columns), sub_rows, sub_cols
    )
    ghost_sets = [
        from_band(spread[band_index(edge_id, rows_ext, cols_ext)], edge_id) for edge_id in range(4)
    ]
    returned = cross(ghost_sets, seam_row, False, offsets, live_edge, panel_side)
    got_left, got_right = neighbours_out(spread[:, tile_width + margin :], spread[:, :margin], 1)
    spread = spread.at[:, margin : 2 * margin].add(jnp.where(left_valid, got_left, 0.0))
    spread = spread.at[:, tile_width : tile_width + margin].add(
        jnp.where(right_valid, got_right, 0.0)
    )
    narrow = spread[:, margin : tile_width + margin]
    got_below, got_above = neighbours_out(narrow[height + margin :], narrow[:margin], tile_cols)
    narrow = narrow.at[margin : 2 * margin].add(got_below)
    narrow = narrow.at[height : height + margin].add(got_above)
    owned_cells = narrow[margin : height + margin]
    for edge_id in range(4):
        edge_part = lax.dynamic_slice_in_dim(
            returned[edge_id // 2], offsets[edge_id], lengths[edge_id], 1
        )
        where_cells = band_index(edge_id, height, tile_width)
        addition = jnp.where(live_edge[edge_id], into_cells(edge_part, edge_id), 0.0)
        owned_cells = owned_cells.at[where_cells].add(addition)
    return owned_cells[None, None]


def solution(mesh):
    placed = (P("panel", "tile", None, None, None), P("panel", "tile", None, None, None), P(), P())
    return jax.shard_map(
        local,
        mesh=mesh,
        in_specs=placed,
        out_specs=P("panel", "tile", None, None, None),
        check_vma=False,
    )
```

profile of v0, /device:TPU:1, one launch (start us, length us, event | category | flops | bytes accessed | tf_op | source)
XLA Modules:
  0.0 259.5 jit_solution(179124195961475757)
XLA Ops:
  6.1 40.0 %all_to_all.30 = bf16[64,64,128]{2,1,0:T(8,128)(2,1)S(1)} all-to-all(bf16[64,64,128]{2,1,0:T(8,128)(2,1)S(1)} %bitcast.235), channel_id=1, replica_groups=mesh['panel'=4,'tile'=64] {'tile'}, dimensions={0} | all-to-all | bytes 2097152 | tf_op jit(solution)/shard_map/all_to_all | solution.py:25
  47.5 7.6 %all-to-all-start.1 = ((bf16[64,64,128]{2,1,0:T(8,128)(2,1)}), bf16[64,64,128]{2,1,0:T(8,128)(2,1)S(1)}, u32[]{:S(2)}, u32[]{:S(2)}) async-start(bf16[64,64,128]{2,1,0:T(8,128)(2,1)} %broadcast_in_dim.35), calls=%async_computation.1 | async-start | bytes 2097152 | tf_op jit(solution)/shard_map/all_to_all | solution.py:36
  58.9 21.6 %all-to-all-done.1 = bf16[64,64,128]{2,1,0:T(8,128)(2,1)S(1)} async-done(((bf16[64,64,128]{2,1,0:T(8,128)(2,1)}), bf16[64,64,128]{2,1,0:T(8,128)(2,1)S(1)}, u32[]{:S(2)}, u32[]{:S(2)}) %all-to-all-start.1) | async-done | bytes 1048608 | tf_op jit(solution)/shard_map/all_to_all | solution.py:36
  80.6 1.6 pad_maximum_fusion
  82.2 8.5 %all-to-all-start.2 = ((bf16[4,8,256,128]{3,2,1,0:T(8,128)(2,1)}), bf16[4,8,256,128]{3,2,1,0:T(8,128)(2,1)S(1)}, u32[]{:S(2)}, u32[]{:S(2)}) async-start(bf16[4,8,256,128]{3,2,1,0:T(8,128)(2,1)} %pad_maximum_fusion), calls=%async_computation.2 | async-start | bytes 4194304 | tf_op jit(solution)/shard_map/all_to_all | solution.py:180
  90.7 3.9 %collective-permute-start = (bf16[8,8,128]{2,1,0:T(8,128)(2,1)S(1)}, bf16[8,8,128]{2,1,0:T(8,128)(2,1)S(1)}, u32[]{:S(2)}, u32[]{:S(2)}) collective-permute-start(bf16[8,8,128]{2,1,0:T(8,128)(2,1)S(1)} %get-tuple-element.301), channel_id=1, source_target_pairs={{0,32},{1,33},{2,34},{3,35},{4,36},{5,37},{6,38},{7,39},{8,40},{9,... | collective-permute-start | bytes 49160 | tf_op jit(solution)/shard_map/ppermute | solution.py:15
  94.6 1.3 collective-permute-start.1
  99.0 1.8 collective-permute-done.1
  106.0 4.7 %collective-permute-start.2 = (bf16[144,8,128]{2,0,1:T(8,128)(2,1)}, bf16[144,8,128]{2,0,1:T(8,128)(2,1)}, u32[]{:S(2)}, u32[]{:S(2)}) collective-permute-start(bf16[144,8,128]{2,0,1:T(8,128)(2,1)} %constant_dynamic-update-slice_fusion), channel_id=1, source_target_pairs={{0,1},{1,2},{2,3},{3,4},{4,5},{5,6},{6,7},{7,8},{8,9},{9,10},{10,1... | collective-permute-start | bytes 884744 | tf_op jit(solution)/shard_map/ppermute | solution.py:15
  111.0 12.2 %all-to-all-done.2 = bf16[4,8,256,128]{3,2,1,0:T(8,128)(2,1)S(1)} async-done(((bf16[4,8,256,128]{3,2,1,0:T(8,128)(2,1)}), bf16[4,8,256,128]{3,2,1,0:T(8,128)(2,1)S(1)}, u32[]{:S(2)}, u32[]{:S(2)}) %all-to-all-start.2) | async-done | bytes 2097184 | tf_op jit(solution)/shard_map/all_to_all | solution.py:180
  129.5 3.3 %broadcast_multiply_fusion = f32[16,128,576]{1,2,0:T(8,128)S(1)} fusion(f32[576]{0:T(1024)S(1)} %copy-done.3, bf16[16,576,128]{2,1,0:T(8,128)(2,1)S(1)} %bitcast.240, bf16[1,1,16,576,576]{4,3,2,1,0:T(8,128)(2,1)S(1)} %bitcast.256), kind=kOutput, calls=%fused_computation.2 | convolution fusion | flops 1360134144 | bytes 17697024 | tf_op jit(solution)/shard_map/noi,nir->nor/dot_general | solution.py:268
  133.0 1.3 fusion.5
  134.3 1.9 fusion.6
  137.5 1.3 collective-permute-start.4
  138.8 1.5 collective-permute-start.5
  140.5 3.9 %collective-permute-done.4 = bf16[144,8,128]{2,0,1:T(8,128)(2,1)S(1)} collective-permute-done((bf16[144,8,128]{2,0,1:T(8,128)(2,1)S(1)}, bf16[144,8,128]{2,0,1:T(8,128)(2,1)S(1)}, u32[]{:S(2)}, u32[]{:S(2)}) %collective-permute-start.4) | collective-permute-done | bytes 294944 | tf_op jit(solution)/shard_map/ppermute | solution.py:15
  144.4 3.9 %collective-permute-done.5 = bf16[144,8,128]{2,0,1:T(8,128)(2,1)S(1)} collective-permute-done((bf16[144,8,128]{2,0,1:T(8,128)(2,1)S(1)}, bf16[144,8,128]{2,0,1:T(8,128)(2,1)S(1)}, u32[]{:S(2)}, u32[]{:S(2)}) %collective-permute-start.5) | collective-permute-done | bytes 294944 | tf_op jit(solution)/shard_map/ppermute | solution.py:15
  148.8 35.2 %all_to_all.31 = bf16[64,64,128]{2,1,0:T(8,128)(2,1)S(1)} all-to-all(bf16[64,64,128]{2,1,0:T(8,128)(2,1)S(1)} %bitcast.236), channel_id=1, replica_groups=mesh['panel'=4,'tile'=64] {'tile'}, dimensions={0} | all-to-all | bytes 2097152 | tf_op jit(solution)/shard_map/all_to_all | solution.py:25
  184.4 32.2 %all_to_all.32 = bf16[64,64,128]{2,1,0:T(8,128)(2,1)S(1)} all-to-all(bf16[64,64,128]{2,1,0:T(8,128)(2,1)S(1)} %broadcast_in_dim.38), channel_id=1, replica_groups=mesh['panel'=4,'tile'=64] {'tile'}, dimensions={0} | all-to-all | bytes 2097152 | tf_op jit(solution)/shard_map/all_to_all | solution.py:36
  217.3 1.6 pad_maximum_fusion.1
  218.9 9.1 %all-to-all-start.5 = ((bf16[4,8,256,128]{3,2,1,0:T(8,128)(2,1)}), bf16[4,8,256,128]{3,2,1,0:T(8,128)(2,1)S(1)}, u32[]{:S(2)}, u32[]{:S(2)}) async-start(bf16[4,8,256,128]{3,2,1,0:T(8,128)(2,1)} %pad_maximum_fusion.1), calls=%async_computation.5 | async-start | bytes 4194304 | tf_op jit(solution)/shard_map/all_to_all | solution.py:185
  228.0 3.9 %collective-permute-start.6 = (bf16[8,8,128]{2,0,1:T(8,128)(2,1)S(1)}, bf16[8,8,128]{2,0,1:T(8,128)(2,1)S(1)}, u32[]{:S(2)}, u32[]{:S(2)}) collective-permute-start(bf16[8,8,128]{2,0,1:T(8,128)(2,1)S(1)} %get-tuple-element.299), channel_id=1, source_target_pairs={{0,32},{1,33},{2,34},{3,35},{4,36},{5,37},{6,38},{7,39},{8,40},{9,... | collective-permute-start | bytes 49160 | tf_op jit(solution)/shard_map/ppermute | solution.py:15
  233.2 5.0 %collective-permute-done.7 = bf16[8,8,128]{2,0,1:T(8,128)(2,1)S(1)} collective-permute-done((bf16[8,8,128]{2,0,1:T(8,128)(2,1)S(1)}, bf16[8,8,128]{2,0,1:T(8,128)(2,1)S(1)}, u32[]{:S(2)}, u32[]{:S(2)}) %collective-permute-start.7) | collective-permute-done | bytes 16416 | tf_op jit(solution)/shard_map/ppermute | solution.py:15
  239.0 15.2 %all-to-all-done.5 = bf16[4,8,256,128]{3,2,1,0:T(8,128)(2,1)S(1)} async-done(((bf16[4,8,256,128]{3,2,1,0:T(8,128)(2,1)}), bf16[4,8,256,128]{3,2,1,0:T(8,128)(2,1)S(1)}, u32[]{:S(2)}, u32[]{:S(2)}) %all-to-all-start.5) | async-done | bytes 2097184 | tf_op jit(solution)/shard_map/all_to_all | solution.py:185
  (127 shorter events, 30.1 us)
Async XLA Ops:
  46.0 9.0 %copy-start.1 = (s32[4,4,3]{1,0,2:T(4,128)S(1)}, s32[4,4,3]{1,0,2:T(4,128)}, u32[]{:S(2)}) copy-start(s32[4,4,3]{1,0,2:T(4,128)} %param.53) | copy-start | bytes 580
  47.5 33.0 %all-to-all-start.1 = ((bf16[64,64,128]{2,1,0:T(8,128)(2,1)}), bf16[64,64,128]{2,1,0:T(8,128)(2,1)S(1)}, u32[]{:S(2)}, u32[]{:S(2)}) async-start(bf16[64,64,128]{2,1,0:T(8,128)(2,1)} %broadcast_in_dim.35), calls=%async_computation.1 | async-start | bytes 2097152 | tf_op jit(solution)/shard_map/all_to_all | solution.py:36
  82.2 23.1 %copy-start.2 = (s32[5]{0:T(128)S(1)}, s32[5]{0:T(128)}, u32[]{:S(2)}) copy-start(s32[5]{0:T(128)} %constant.678.clone.1) | copy-start | bytes 64
  82.2 41.0 %all-to-all-start.2 = ((bf16[4,8,256,128]{3,2,1,0:T(8,128)(2,1)}), bf16[4,8,256,128]{3,2,1,0:T(8,128)(2,1)S(1)}, u32[]{:S(2)}, u32[]{:S(2)}) async-start(bf16[4,8,256,128]{3,2,1,0:T(8,128)(2,1)} %pad_maximum_fusion), calls=%async_computation.2 | async-start | bytes 4194304 | tf_op jit(solution)/shard_map/all_to_all | solution.py:180
  90.7 7.0 %collective-permute-start = (bf16[8,8,128]{2,1,0:T(8,128)(2,1)S(1)}, bf16[8,8,128]{2,1,0:T(8,128)(2,1)S(1)}, u32[]{:S(2)}, u32[]{:S(2)}) collective-permute-start(bf16[8,8,128]{2,1,0:T(8,128)(2,1)S(1)} %get-tuple-element.301), channel_id=1, source_target_pairs={{0,32},{1,33},{2,34},{3,35},{4,36},{5,37},{6,38},{7,39},{8,40},{9,... | collective-permute-start | bytes 49160 | tf_op jit(solution)/shard_map/ppermute | solution.py:15
  94.6 6.3 %collective-permute-start.1 = (bf16[8,8,128]{2,0,1:T(8,128)(2,1)S(1)}, bf16[8,8,128]{2,0,1:T(8,128)(2,1)S(1)}, u32[]{:S(2)}, u32[]{:S(2)}) collective-permute-start(bf16[8,8,128]{2,0,1:T(8,128)(2,1)S(1)} %bitcast.251), channel_id=1, source_target_pairs={{32,0},{33,1},{34,2},{35,3},{36,4},{37,5},{38,6},{39,7},{40,8},{41... | collective-permute-start | bytes 49160 | tf_op jit(solution)/shard_map/ppermute | solution.py:15
  101.4 9.5 %collective-permute-start.3 = (bf16[144,8,128]{2,0,1:T(8,128)(2,1)}, bf16[144,8,128]{2,0,1:T(8,128)(2,1)S(1)}, u32[]{:S(2)}, u32[]{:S(2)}) collective-permute-start(bf16[144,8,128]{2,0,1:T(8,128)(2,1)} %constant_dynamic-update-slice_fusion), channel_id=1, source_target_pairs={{1,0},{2,1},{3,2},{4,3},{5,4},{6,5},{7,6},{8,7},{9,8},{10,9},{11,1... | collective-permute-start | bytes 884744 | tf_op jit(solution)/shard_map/ppermute | solution.py:15
  106.0 18.6 %collective-permute-start.2 = (bf16[144,8,128]{2,0,1:T(8,128)(2,1)}, bf16[144,8,128]{2,0,1:T(8,128)(2,1)}, u32[]{:S(2)}, u32[]{:S(2)}) collective-permute-start(bf16[144,8,128]{2,0,1:T(8,128)(2,1)} %constant_dynamic-update-slice_fusion), channel_id=1, source_target_pairs={{0,1},{1,2},{2,3},{3,4},{4,5},{5,6},{6,7},{7,8},{8,9},{9,10},{10,1... | collective-permute-start | bytes 884744 | tf_op jit(solution)/shard_map/ppermute | solution.py:15
  124.4 3.4 %slice-start = ((s8[11796480]{0:T(1024)(128)(4,1)}), s8[4194304]{0:T(1024)(128)(4,1)S(1)}, s32[]{:S(2)}) async-start(s8[11796480]{0:T(1024)(128)(4,1)} %bitcast.255), calls=%async_computation.6 | async-start | bytes 8388608
  126.1 2.3 slice-start.1
  126.9 2.5 slice-start.2
  127.4 2.1 copy-start.3
  137.5 7.0 %collective-permute-start.4 = (bf16[144,8,128]{2,0,1:T(8,128)(2,1)S(1)}, bf16[144,8,128]{2,0,1:T(8,128)(2,1)S(1)}, u32[]{:S(2)}, u32[]{:S(2)}) collective-permute-start(bf16[144,8,128]{2,0,1:T(8,128)(2,1)S(1)} %get-tuple-element.288), channel_id=1, source_target_pairs={{0,1},{1,2},{2,3},{3,4},{4,5},{5,6},{6,7},{7,8},{8,9},{9,10},{10,1... | collective-permute-start | bytes 884744 | tf_op jit(solution)/shard_map/ppermute | solution.py:15
  138.8 9.5 %collective-permute-start.5 = (bf16[144,8,128]{2,0,1:T(8,128)(2,1)S(1)}, bf16[144,8,128]{2,0,1:T(8,128)(2,1)S(1)}, u32[]{:S(2)}, u32[]{:S(2)}) collective-permute-start(bf16[144,8,128]{2,0,1:T(8,128)(2,1)S(1)} %get-tuple-element.289), channel_id=1, source_target_pairs={{1,0},{2,1},{3,2},{4,3},{5,4},{6,5},{7,6},{8,7},{9,8},{10,9},{11,1... | collective-permute-start | bytes 884744 | tf_op jit(solution)/shard_map/ppermute | solution.py:15
  218.9 35.3 %all-to-all-start.5 = ((bf16[4,8,256,128]{3,2,1,0:T(8,128)(2,1)}), bf16[4,8,256,128]{3,2,1,0:T(8,128)(2,1)S(1)}, u32[]{:S(2)}, u32[]{:S(2)}) async-start(bf16[4,8,256,128]{3,2,1,0:T(8,128)(2,1)} %pad_maximum_fusion.1), calls=%async_computation.5 | async-start | bytes 4194304 | tf_op jit(solution)/shard_map/all_to_all | solution.py:185
  228.0 5.2 %collective-permute-start.6 = (bf16[8,8,128]{2,0,1:T(8,128)(2,1)S(1)}, bf16[8,8,128]{2,0,1:T(8,128)(2,1)S(1)}, u32[]{:S(2)}, u32[]{:S(2)}) collective-permute-start(bf16[8,8,128]{2,0,1:T(8,128)(2,1)S(1)} %get-tuple-element.299), channel_id=1, source_target_pairs={{0,32},{1,33},{2,34},{3,35},{4,36},{5,37},{6,38},{7,39},{8,40},{9,... | collective-permute-start | bytes 49160 | tf_op jit(solution)/shard_map/ppermute | solution.py:15
  231.9 6.3 %collective-permute-start.7 = (bf16[8,8,128]{2,0,1:T(8,128)(2,1)S(1)}, bf16[8,8,128]{2,0,1:T(8,128)(2,1)S(1)}, u32[]{:S(2)}, u32[]{:S(2)}) collective-permute-start(bf16[8,8,128]{2,0,1:T(8,128)(2,1)S(1)} %get-tuple-element.298), channel_id=1, source_target_pairs={{32,0},{33,1},{34,2},{35,3},{36,4},{37,5},{38,6},{39,7},{40,8},{41... | collective-permute-start | bytes 49160 | tf_op jit(solution)/shard_map/ppermute | solution.py:15
  256.0 1.0 copy-start
where the time goes:
time: 260 us
  blocking collectives  107 us (41%)
  waiting for transfers between devices  63.8 us (25%)
  starting transfers between devices  44.3 us (17%)
  local copies, waits for them, and re-layouts  18.8 us (7%)
  other arithmetic  14.8 us (6%)
  between operations  7.19 us (3%)
  matrix products  3.27 us (1%)
    all_to_all x2, blocking collectives, summed_on_arrival(): lax.all_to_all(in_blocks(value, dim, peers), axis, 0, 0, tiled=True)  75.2 us
    all_to_all x1, blocking collectives, copy_for_each(): lax.all_to_all(jnp.broadcast_to(value[None], (peers, *value.shape)), axis...  32.2 us
    all_to_all x1, waiting for transfers between devices, copy_for_each(): lax.all_to_all(jnp.broadcast_to(value[None], (peers, *value.shape)), axis...  21.6 us
    ppermute x8, starting transfers between devices, passed_along(): return lax.ppermute(block, axis, route)  19.1 us
    all_to_all x1, waiting for transfers between devices, cross(): lax.all_to_all(outgoing_of(totals, slot_facts).astype(jnp.bfloat16), 'pan...  15.2 us
    ppermute x8, waiting for transfers between devices, passed_along(): return lax.ppermute(block, axis, route)  14.8 us
    all_to_all x1, waiting for transfers between devices, cross(): lax.all_to_all(outgoing_of(totals, slot_facts), 'panel', split_axis=0, co...  12.2 us
    all_to_all x1, starting transfers between devices, cross(): lax.all_to_all(outgoing_of(totals, slot_facts).astype(jnp.bfloat16), 'pan...  9.09 us
  transfers between devices with their start and end apart: 11, of which 8 were waited for; matrix products, arithmetic and copies ran while one was open for 4% of the time, Pallas kernels for 0%

commit v1 on v0

v1 whole, which is shorter than its diff:
```python
import functools

import jax
import jax.numpy as jnp
from jax import lax
from jax.experimental import pallas as pl
from jax.experimental.pallas import tpu as pltpu
from jax.sharding import PartitionSpec as P

PANELS = 4
TILE_COLS = 32
H = 128
LAST = TILE_COLS - 1
NSUB = 16
CELLS = 576
MESH = pl.DeviceIdType.MESH

SEND_COUNT = 80
RECV_COUNT = 80


def kernel(seam, res_hbm, inv_hbm, weight, out_hbm, res, inv, wrep, ext, spread, spb, out,
           s1buf, send_x, recv_x, row_buf, col_buf, yf, gf,
           from_left, from_right, from_vert, from_dl, from_dr,
           home_left, home_right, home_corner, send_b, recv_b, cb_buf, corner_in,
           local_sem, inv_sem, send_sem, recv_sem):
    panel = lax.axis_index("panel")
    tile = lax.axis_index("tile")
    r = tile // TILE_COLS
    c = tile % TILE_COLS
    other = 1 - r
    has_left = c > 0
    has_right = c < LAST
    at_end = jnp.logical_or(c == 0, c == LAST)
    side = jnp.where(c == LAST, 1, 0)
    half = c // 16
    is_self = jnp.logical_or(tile == 0, tile == 2 * TILE_COLS - 1)
    seam_rows = 136 * r
    inner_rows = 136 * other
    two_corners = jnp.logical_or(c == 15, c == 16)
    corner_tile = half * TILE_COLS + LAST * r
    other_corner = (1 - half) * TILE_COLS + LAST * r

    def tid(row, col):
        return row * TILE_COLS + col

    res_copy = pltpu.make_async_copy(res_hbm, res, local_sem.at[0])
    res_copy.start()
    for n in range(NSUB):
        pltpu.make_async_copy(inv_hbm.at[n], inv.at[n], inv_sem.at[n]).start()

    zero_block = jnp.zeros((8, 8, 128), jnp.bfloat16)

    @pl.when(at_end)
    def _():
        ext[pl.ds(seam_rows, 8), 2 * side] = zero_block

    home_corner[...] = jnp.zeros_like(home_corner)
    home_left[...] = zero_block
    home_right[...] = zero_block

    barrier = pltpu.get_barrier_semaphore()

    def greet(cond, pan, til):
        @pl.when(cond)
        def _():
            pl.semaphore_signal(barrier, inc=1, device_id=(pan, til), device_id_type=MESH)

    yes = tile >= 0
    greet(has_left, panel, tid(r, c - 1))
    greet(has_right, panel, tid(r, c + 1))
    greet(yes, panel, tid(other, c))
    greet(has_left, panel, tid(other, c - 1))
    greet(has_right, panel, tid(other, c + 1))
    for step in range(1, PANELS):
        q = lax.rem(panel + step, PANELS)
        for row in range(2):
            greet(yes, q, tid(row, c))
            greet(yes, q, tid(row, LAST - c))
    greet(jnp.logical_not(is_self), panel, corner_tile)
    greet(two_corners, panel, other_corner)
    for jj in range(18):
        k = 16 * r + jj - 1
        ok = jnp.logical_and(at_end, jnp.logical_and(k >= 0, k < TILE_COLS))
        ok = jnp.logical_and(ok, tid(side, k) != tile)
        greet(ok, panel, tid(side, k))

    res_copy.wait()
    ext[8:136, 1] = res[...].astype(jnp.bfloat16)

    count = 13 + 2 * has_left.astype(jnp.int32) + 2 * has_right.astype(jnp.int32)
    count = count + jnp.where(is_self, 0, 1) + jnp.where(two_corners, 1, 0)
    count = count + jnp.where(at_end, jnp.where(is_self, 16, 17), 0)
    pl.semaphore_wait(barrier, count)

    sends = []

    def remote(src, dst, slot, rslot, pan, til):
        return pltpu.make_async_remote_copy(
            src_ref=src, dst_ref=dst, send_sem=send_sem.at[slot], recv_sem=recv_sem.at[rslot],
            device_id=(pan, til), device_id_type=MESH)

    def send(cond, src, dst, slot, rslot, pan, til):
        @pl.when(cond)
        def _():
            remote(src, dst, slot, rslot, pan, til).start()
        sends.append((cond, src, dst, slot, rslot, pan, til))

    def arrived(cond, dst, rslot):
        @pl.when(cond)
        def _():
            remote(dst, dst, 0, rslot, panel, tile).wait_recv()

    for j in range(16):
        home = tid(side, 16 * r + j)
        ok = jnp.logical_and(at_end, home != tile)
        send(ok, ext.at[pl.ds(8 + 8 * j, 8), 1], s1buf, j, 0, panel, home)
    edge_src = ext.at[pl.ds(128 - 120 * r, 8), 1]
    send(yes, edge_src, ext.at[pl.ds(136 * r, 8), 1], 16, 1, panel, tid(other, c))
    send(has_right, edge_src, ext.at[pl.ds(136 * r, 8), 0], 17, 2, panel, tid(other, c + 1))
    send(has_left, edge_src, ext.at[pl.ds(136 * r, 8), 2], 18, 3, panel, tid(other, c - 1))
    mid = ext.at[pl.ds(8, 128), 1]
    send(has_right, mid, ext.at[pl.ds(8, 128), 0], 19, 4, panel, tid(r, c + 1))
    send(has_left, mid, ext.at[pl.ds(8, 128), 2], 20, 5, panel, tid(r, c - 1))

    row_type = jnp.where(seam[panel, 1, 0] >= 0, 1, 0)
    edge = 2 * r + row_type
    facing_panel = jnp.maximum(seam[panel, edge, 0], 0)
    rev = jnp.where(seam[panel, edge, 2] > 0, 1, 0)
    facing = lax.rem(edge + 2 + seam[panel, edge, 1], 4)
    facing_slot = jnp.where(facing >= 2, 1, 0)
    facing_row = facing - 2 * facing_slot
    delta = lax.rem(facing_panel - panel + 3, 4)
    delta = jnp.clip(delta, 0, 2)
    pick = (delta * 2 + facing_slot) * 2 + rev
    along = jnp.where(facing_row == 1, 1, 8)
    across = jnp.where(facing_row == 1, 8, 1)
    flip = jnp.where(facing_slot == r, 1, 0)
    along_step = along * (1 - 2 * rev)
    across_step = across * (1 - 2 * flip)
    start = along * 7 * rev + across * 7 * flip
    step_i = jnp.where(row_type == 1, across_step, along_step)
    step_j = jnp.where(row_type == 1, along_step, across_step)

    def turned(received):
        yf[...] = received[pick].astype(jnp.float32).reshape(64, 128)
        for i in range(8):
            for j in range(8):
                gf[pl.ds(8 * i + j, 1), :] = yf[pl.ds(start + step_i * i + step_j * j, 1), :]
        return gf[...].reshape(8, 8, 128)

    own_rows = ext[pl.ds(8 + 120 * r, 8), 1]

    @pl.when(is_self)
    def _():
        s1buf[...] = own_rows

    arrived(jnp.logical_not(is_self), s1buf, 0)
    rowf = jnp.full((8, 8, 128), row_type, jnp.int32) == 1
    send_x[...] = jnp.where(rowf, own_rows.astype(jnp.float32), s1buf[...].astype(jnp.float32)).astype(jnp.bfloat16)

    def across_panels(buf, landing, base, rbase):
        slot = 0
        for step in range(1, PANELS):
            q = lax.rem(panel + step, PANELS)
            for row in range(2):
                for v in range(2):
                    col = LAST - c if v else c
                    for own in range(2):
                        idx = ((3 - step) * 2 + own) * 2 + v
                        if own == 0:
                            send(jnp.logical_and(yes, r == 0), buf, landing.at[idx],
                                 base + slot, rbase + idx, q, tid(row, col))
                        else:
                            send(r == 1, buf, landing.at[idx],
                                 base + slot, rbase + idx, q, tid(row, col))
                    slot += 1
        for idx in range(12):
            arrived(yes, landing.at[idx], rbase + idx)

    across_panels(send_x, recv_x, 21, 6)
    turn = turned(recv_x)
    zero_f = jnp.zeros((8, 8, 128), jnp.float32)
    row_val = jnp.where(rowf, turn, zero_f).astype(jnp.bfloat16)
    row_buf[...] = row_val
    col_buf[...] = jnp.where(rowf, zero_f, turn).astype(jnp.bfloat16)
    pos = 8 + 8 * (c - 16 * half)
    send(jnp.logical_not(is_self), col_buf, ext.at[pl.ds(pos, 8), 2 * r], 33, 20 + c - 16 * half, panel, corner_tile)
    opos = 8 + 8 * (c - 16 * (1 - half))
    send(two_corners, col_buf, ext.at[pl.ds(opos, 8), 2 * r], 34, 20 + c - 16 * (1 - half), panel, other_corner)
    send(has_right, row_buf, ext.at[pl.ds(seam_rows, 8), 0], 35, 18, panel, tid(r, c + 1))
    send(has_left, row_buf, ext.at[pl.ds(seam_rows, 8), 2], 36, 37, panel, tid(r, c - 1))
    ext[pl.ds(seam_rows, 8), 1] = row_val

    @pl.when(is_self)
    def _():
        ext[pl.ds(pos, 8), 2 * r] = col_buf[...]

    wrep[...] = jnp.transpose(jnp.broadcast_to(weight[...], (128, CELLS)), (1, 0))
    spread[...] = jnp.zeros_like(spread)

    arrived(yes, ext.at[pl.ds(inner_rows, 8), 1], 1)
    arrived(has_left, ext.at[pl.ds(inner_rows, 8), 0], 2)
    arrived(has_right, ext.at[pl.ds(inner_rows, 8), 2], 3)
    arrived(has_left, ext.at[pl.ds(8, 128), 0], 4)
    arrived(has_right, ext.at[pl.ds(8, 128), 2], 5)
    arrived(has_left, ext.at[pl.ds(seam_rows, 8), 0], 18)
    arrived(has_right, ext.at[pl.ds(seam_rows, 8), 2], 37)
    for jj in range(18):
        k = 16 * r + jj - 1
        ok = jnp.logical_and(at_end, jnp.logical_and(k >= 0, k < TILE_COLS))
        ok = jnp.logical_and(ok, tid(side, k) != tile)
        arrived(ok, ext.at[pl.ds(8 * jj, 8), 2 * side], 19 + jj)

    flat = ext.reshape(144 * 24, 128)
    def solve(n, carry):
        pltpu.make_async_copy(inv_hbm.at[n], inv.at[n], inv_sem.at[n]).wait()
        rows = pl.ds(pl.multiple_of(n * 192, 64), CELLS)
        solved = jnp.dot(inv[n], flat[rows, :], preferred_element_type=jnp.float32)
        spread[rows, :] += solved * wrep[...]
        return carry

    lax.fori_loop(0, NSUB, solve, 0)

    cube = spread.reshape(144, 3, 8, 128)
    spb[...] = cube[...].astype(jnp.bfloat16)

    for jj in range(18):
        k = 16 * r + jj - 1
        ok = jnp.logical_and(at_end, jnp.logical_and(k >= 0, k < TILE_COLS))
        mine = tid(side, k) == tile
        send(jnp.logical_and(ok, jnp.logical_not(mine)), spb.at[pl.ds(8 * jj, 8), 2 * side],
             home_corner.at[r], 37 + jj, 38 + r, panel, tid(side, k))
    send(has_left, spb.at[pl.ds(seam_rows, 8), 0], home_right, 55, 40, panel, tid(r, c - 1))
    send(has_right, spb.at[pl.ds(seam_rows, 8), 2], home_left, 56, 41, panel, tid(r, c + 1))
    send(has_left, spb.at[pl.ds(8, 128), 0], from_right, 57, 42, panel, tid(r, c - 1))
    send(has_right, spb.at[pl.ds(8, 128), 2], from_left, 58, 43, panel, tid(r, c + 1))
    send(yes, spb.at[pl.ds(inner_rows, 8), 1], from_vert, 59, 44, panel, tid(other, c))
    send(has_left, spb.at[pl.ds(inner_rows, 8), 0], from_dr, 60, 45, panel, tid(other, c - 1))
    send(has_right, spb.at[pl.ds(inner_rows, 8), 2], from_dl, 61, 46, panel, tid(other, c + 1))

    @pl.when(is_self)
    def _():
        home_corner[r] = spb[pl.ds(pos, 8), 2 * r]

    first_corner = jnp.logical_or(c <= 15, c == 16)
    second_corner = jnp.logical_or(c >= 16, c == 15)
    arrived(jnp.logical_and(first_corner, tile != 0), home_corner.at[0], 38)
    arrived(jnp.logical_and(second_corner, tile != 2 * TILE_COLS - 1), home_corner.at[1], 39)
    arrived(has_right, home_right, 40)
    arrived(has_left, home_left, 41)
    f32 = jnp.float32
    by_row = cube[pl.ds(seam_rows, 8), 1] + home_left[...].astype(f32) + home_right[...].astype(f32)
    by_col = home_corner[0].astype(f32) + home_corner[1].astype(f32)
    send_b[...] = jnp.where(rowf, by_row, by_col).astype(jnp.bfloat16)
    across_panels(send_b, recv_b, 62, 47)
    turn = turned(recv_b)
    cb_buf[...] = jnp.where(rowf, zero_f, turn).astype(jnp.bfloat16)
    seam_add = jnp.where(rowf, turn, zero_f)
    send(jnp.logical_not(is_self), cb_buf, corner_in.at[pl.ds(8 * (c - 16 * half), 8)], 74,
         59 + c - 16 * half, panel, corner_tile)

    arrived(has_right, from_right, 42)
    arrived(has_left, from_left, 43)
    arrived(yes, from_vert, 44)
    arrived(has_right, from_dr, 45)
    arrived(has_left, from_dl, 46)
    out[...] = cube[pl.ds(8, 128), 1]

    @pl.when(has_right)
    def _():
        out[...] += from_right[...].astype(f32)
        out[pl.ds(120 * other, 8)] += from_dr[...].astype(f32)

    @pl.when(has_left)
    def _():
        out[...] += from_left[...].astype(f32)
        out[pl.ds(120 * other, 8)] += from_dl[...].astype(f32)

    out[pl.ds(120 * other, 8)] += from_vert[...].astype(f32)
    out[pl.ds(120 * r, 8)] += seam_add

    @pl.when(is_self)
    def _():
        corner_in[pl.ds(8 * (c - 16 * half), 8)] = cb_buf[...]

    for j in range(16):
        home = tid(side, 16 * r + j)
        arrived(jnp.logical_and(at_end, home != tile), corner_in.at[pl.ds(8 * j, 8)], 59 + j)

    @pl.when(at_end)
    def _():
        out[...] += corner_in[...].astype(f32)

    out_copy = pltpu.make_async_copy(out, out_hbm, local_sem.at[1])
    out_copy.start()
    for cond, src, dst, slot, rslot, pan, til in sends:
        @pl.when(cond)
        def _():
            remote(src, dst, slot, rslot, pan, til).wait_send()
    out_copy.wait()


def local(residual, inverse, blend_weight, seam_table):
    bf16, f32 = jnp.bfloat16, jnp.float32
    chunk = pltpu.VMEM((8, 8, 128), bf16)
    scratch = [
        pltpu.VMEM((H, 8, 128), f32),
        pltpu.VMEM((NSUB, CELLS, CELLS), bf16),
        pltpu.VMEM((CELLS, 128), f32),
        pltpu.VMEM((144, 3, 8, 128), bf16),
        pltpu.VMEM((144 * 24, 128), f32),
        pltpu.VMEM((144, 3, 8, 128), bf16),
        pltpu.VMEM((H, 8, 128), f32),
        chunk,
        chunk,
        pltpu.VMEM((12, 8, 8, 128), bf16),
        chunk, chunk,
        pltpu.VMEM((64, 128), f32), pltpu.VMEM((64, 128), f32),
        pltpu.VMEM((H, 8, 128), bf16), pltpu.VMEM((H, 8, 128), bf16),
        chunk, chunk, chunk,
        chunk, chunk,
        pltpu.VMEM((2, 8, 8, 128), bf16),
        chunk,
        pltpu.VMEM((12, 8, 8, 128), bf16),
        chunk,
        pltpu.VMEM((H, 8, 128), bf16),
        pltpu.SemaphoreType.DMA((2,)),
        pltpu.SemaphoreType.DMA((NSUB,)),
        pltpu.SemaphoreType.DMA((SEND_COUNT,)),
        pltpu.SemaphoreType.DMA((RECV_COUNT,)),
    ]
    any_space = pl.BlockSpec(memory_space=pl.ANY)
    out = pl.pallas_call(
        kernel,
        out_shape=jax.ShapeDtypeStruct((H, 8, 128), f32),
        in_specs=[pl.BlockSpec(memory_space=pltpu.SMEM), any_space, any_space,
                  pl.BlockSpec(memory_space=pltpu.VMEM)],
        out_specs=any_space,
        scratch_shapes=scratch,
        compiler_params=pltpu.CompilerParams(
            collective_id=0, has_side_effects=True, vmem_limit_bytes=56 * 1024 * 1024),
        name="schwarz",
    )(seam_table, residual[0, 0], inverse[0, 0], blend_weight.reshape(1, CELLS))
    return out[None, None]


def solution(mesh):
    placed = (P("panel", "tile", None, None, None), P("panel", "tile", None, None, None), P(), P())
    return jax.shard_map(
        local,
        mesh=mesh,
        in_specs=placed,
        out_specs=P("panel", "tile", None, None, None),
        check_vma=False,
    )
```

time: 260 us -> 63.8 us (0.25)
  the two profiles are of different devices: /device:TPU:1 before, /device:TPU:17 now
where the time goes in v1:
time: 63.8 us; the launch traced here: 63.6 us
  Pallas kernels  59.1 us (93%)
  local copies, waits for them, and re-layouts  4.54 us (7%)
    pallas_call x1, Pallas kernels, local(): pl.pallas_call(kernel, out_shape=jax.ShapeDtypeStruct((H, 8, 128), f32),...  59.1 us
    unnamed x2, local copies, waits for them, and re-layouts  3.25 us
    reshape x1, local copies, waits for them, and re-layouts, local(): blend_weight.reshape(1, CELLS)  1.28 us

profile of v1, /device:TPU:17, one launch (start us, length us, event | category | flops | bytes accessed | tf_op | source)
XLA Modules:
  0.0 63.6 jit_solution(1160117913419636456)
XLA Ops:
  0.0 1.3 %reshape.3.weight = f32[1,576]{1,0:T(1,128)} reshape(f32[576]{0:T(1024)} %param.6) | data formatting | bytes 4608 | tf_op jit(solution)/shard_map/reshape | solution.py:344
  1.3 1.4 %copy.5.seam = s32[4,4,3]{2,1,0:T(4,128)} copy(s32[4,4,3]{1,0,2:T(4,128)} %param.7) | data formatting | bytes 384 | tf_op args[3]
  2.7 59.1 %schwarz.1 = f32[128,8,128]{2,1,0:T(8,128)} custom-call(s32[4,4,3]{2,1,0:T(4,128)} %copy.5.seam, f32[128,8,128]{2,1,0:T(8,128)} %bitcast.5, bf16[16,576,576]{2,1,0:T(8,128)(2,1)} %bitcast.3, f32[1,576]{1,0:T(1,128)} %reshape.3.weight), custom_call_target="tpu_custom_call" | custom-call | tf_op jit(solution)/shard_map/schwarz/pallas_call | solution.py:334
  61.7 1.9 %copy.7 = f32[1,1,128,8,128]{4,3,2,1,0:T(8,128)} copy(f32[1,1,128,8,128]{4,3,2,1,0:T(8,128)} %bitcast.4) | data formatting | bytes 1048576

commit v2 on v1

v2 whole, which is shorter than its diff:
```python
import jax
import jax.numpy as jnp
from jax import lax
from jax.experimental import pallas as pl
from jax.experimental.pallas import tpu as pltpu
from jax.sharding import PartitionSpec as P

PANELS = 4
TILE_COLS = 32
H = 128
LAST = TILE_COLS - 1
NSUB = 16
CELLS = 576
MESH = pl.DeviceIdType.MESH
SENDS = 130
BF16, F32 = jnp.bfloat16, jnp.float32

HALO, HALO_BACK = 0, 5
IN_HOME, CROSS, CROSS_BACK = 10, 18, 21
ROW_GHOST, COL_GHOST = 24, 30
ROW_BACK, COL_BACK = 66, 78
ROW_OWN, COL_OWN = 86, 88
RECVS = 120


def home_of(mu, part):
    z, x = mu % 8, mu // 8
    low = min(z, 7 - z)
    inner = low in (0, 3)
    col = (1 if inner else 0) if z < 4 else (6 if inner else 7)
    return (2 * (low // 2) + part) * 16 + (x ^ part) * 8 + (7 - col if part else col)


def home_at(mu, part):
    z, x = lax.rem(mu, 8), mu // 8
    low = jnp.minimum(z, 7 - z)
    inner = jnp.where(jnp.logical_or(low == 0, low == 3), 1, 0)
    col = jnp.where(z < 4, inner, 7 - inner)
    up = low // 2
    if part:
        return (2 * up + 1) * 16 + (1 - x) * 8 + 7 - col
    return (2 * up) * 16 + x * 8 + col


def kernel(seam, res, inv_hbm, weight, out, inv, ends, wrep, ext, spread, colg, colb, sides, inners, tr, rowg, rowt, own_back, corner_in,
           in_home, cross_out, cross_in, row_out, col_out, row_back, col_back, back_out, back_in,
           xf, yf, zf, rg, from_left, from_right, from_vert, from_dl, from_dr, inv_sem, send_sem, recv_sem):
    panel = lax.axis_index("panel")
    tile = lax.axis_index("tile")
    r = tile // TILE_COLS
    c = lax.rem(tile, TILE_COLS)
    other = 1 - r
    has_left = c > 0
    has_right = c < LAST
    at_end = jnp.logical_or(c == 0, c == LAST)
    side = jnp.where(c == LAST, 1, 0)
    half = c // 16
    seam_rows = 136 * r
    inner_rows = 136 * other
    yes = tile >= 0

    ty, tx, tz = tile // 16, lax.rem(tile // 8, 2), lax.rem(tile, 8)
    part = lax.rem(ty, 2)
    z0 = jnp.where(part == 1, 7 - tz, tz)
    is_home = jnp.logical_or(tz < 2, tz > 5)
    inner = jnp.where(jnp.logical_or(tz == 1, tz == 6), 1, 0)
    up = ty // 2
    low = 2 * up + jnp.where(up == inner, 1, 0)
    mu = 8 * jnp.where(part == 1, 1 - tx, tx) + jnp.where(z0 < 4, low, 7 - low)
    middle = mu == 15

    def tid(row, col):
        return row * TILE_COLS + col

    def chunk_home(k, piece):
        first = k < 16
        m = jnp.where(first, k, LAST - k)
        a, b = home_at(m, 0), home_at(m, 1)
        return jnp.where(first, (a, b)[piece], (b, a)[piece])

    def end_home(j, piece):
        def fixed(k):
            if k < 0 or k > LAST:
                return -1
            m = k if k < 16 else LAST - k
            return home_of(m, piece if k < 16 else 1 - piece)
        return jnp.where(r == 0, fixed(j), fixed(16 + j))

    for n in range(NSUB):
        pltpu.make_async_copy(inv_hbm.at[n], inv.at[n], inv_sem.at[n]).start()

    @pl.when(at_end)
    def _():
        colg[...] = jnp.zeros_like(colg)
        rowg[...] = jnp.zeros_like(rowg)

    @pl.when(is_home)
    def _():
        row_back[...] = jnp.zeros_like(row_back)
        col_back[...] = jnp.zeros_like(col_back)

    barrier = pltpu.get_barrier_semaphore()
    greeted = [jnp.int32(0)]

    def signal(cond, pan, til):
        def now():
            pl.semaphore_signal(barrier, inc=1, device_id=(pan, til), device_id_type=MESH)
        if cond is None:
            now()
        else:
            pl.when(cond)(now)

    def greet(cond, pan, til):
        signal(cond, pan, til)
        greeted[0] = greeted[0] + cond.astype(jnp.int32)

    def both(a, *b):
        for x in b:
            a = jnp.logical_and(a, x)
        return a

    def within(k):
        return jnp.logical_and(k >= 0, k < TILE_COLS)

    served_rows = []
    for slot in range(2):
        for high in range(2):
            k = (LAST - mu) if high else mu
            for b in range(3):
                col = k + 1 - b
                served_rows.append((slot, high, b, tid(slot, col), both(is_home, within(col))))
    served_ends = []
    lowpos, highpos = 8 * mu + 4 * part, 8 * (15 - mu) + 4 * (1 - part)
    for slot in range(2):
        served_ends.append((slot, 0, 0, tid(0, LAST * slot), is_home, 8 + lowpos))
        served_ends.append((slot, 1, 1, tid(1, LAST * slot), is_home, 8 + highpos))
        served_ends.append((slot, 0, 1, tid(1, LAST * slot), both(is_home, middle), 4 * part))
        served_ends.append((slot, 1, 0, tid(0, LAST * slot), both(is_home, middle), 136 + 4 * (1 - part)))
    tile_homes = []
    for b in range(3):
        for piece in range(2):
            k = c + b - 1
            tile_homes.append((b, piece, chunk_home(k, piece), within(k)))
    end_homes = []
    for jj in range(18):
        for piece in range(2):
            home = end_home(jj - 1, piece)
            end_homes.append((jj, piece, home, both(at_end, home >= 0)))

    greet(has_left, panel, tid(r, c - 1))
    greet(has_right, panel, tid(r, c + 1))
    greet(yes, panel, tid(other, c))
    greet(has_left, panel, tid(other, c - 1))
    greet(has_right, panel, tid(other, c + 1))
    for _, _, home, cond in tile_homes:
        greet(both(cond, home != tile), panel, home)

    @pl.when(is_home)
    def _():
        for _, _, _, til, cond in served_rows:
            signal(both(cond, til != tile), panel, til)
        for _, _, _, til, cond, _ in served_ends:
            signal(both(cond, til != tile), panel, til)
        for step in range(1, PANELS):
            signal(None, lax.rem(panel + step, PANELS), tile)

    @pl.when(at_end)
    def _():
        for jj, _, home, cond in end_homes:
            signal(both(cond, home != tile), panel, home)

    for _, _, _, til, cond in served_rows:
        greeted[0] = greeted[0] + both(cond, til != tile).astype(jnp.int32)
    for _, _, _, til, cond, _ in served_ends:
        greeted[0] = greeted[0] + both(cond, til != tile).astype(jnp.int32)
    for _, _, home, cond in end_homes:
        greeted[0] = greeted[0] + both(cond, home != tile).astype(jnp.int32)
    greeted[0] = greeted[0] + jnp.where(is_home, 3, 0)

    ext[8:136, 1] = res[...].astype(BF16)
    for b in range(3):
        ext[pl.ds(seam_rows, 8), b] = jnp.zeros((8, 8, 128), BF16)

    @pl.when(at_end)
    def _():
        for i in range(0, 144, 16):
            ext[i:i + 16, 2 * side] = jnp.zeros((16, 8, 128), BF16)
    xf[...] = res[pl.ds(120 * r, 8)].reshape(64, 128)
    for p in range(8):
        tr[p] = xf[pl.ds(p, 8, stride=8), :].astype(BF16)

    row_type = jnp.where(seam[0, panel, 1] >= 0, 1, 0)
    facts = []
    for slot in range(2):
        edge = 2 * slot + row_type
        facing_panel = jnp.maximum(seam[0, panel, edge], 0)
        facing = lax.rem(edge + 2 + seam[1, panel, edge], 4)
        rev = jnp.where(seam[2, panel, edge] > 0, 1, 0)
        flip = jnp.where((facing >= 2) == (slot == 1), 1, 0)
        pick = jnp.clip(lax.rem(facing_panel - panel + 3, 4), 0, 2)
        facts.append((pick, rev, flip))
    rowf = jnp.full((64, 128), row_type, jnp.int32) == 1
    to_second = [jnp.where(seam[0, panel, 2 + row_type] == lax.rem(panel + step, PANELS), 1, 0)
                 for step in range(1, PANELS)]

    pl.semaphore_wait(barrier, greeted[0])

    def remote(src, dst, slot, rslot, pan, til):
        return pltpu.make_async_remote_copy(
            src_ref=src, dst_ref=dst, send_sem=send_sem.at[slot], recv_sem=recv_sem.at[rslot],
            device_id=(pan, til), device_id_type=MESH)

    used = [0]
    stand_in = {4: tr.at[pl.ds(0, 4)], 8: tr, 128: corner_in, 2: cross_out.at[0]}

    def send(cond, src, dst, rslot, til, pan=None):
        pan = panel if pan is None else pan
        slot = used[0]
        used[0] += 1

        def now():
            remote(src, dst, slot, rslot, pan, til).start()
        if cond is None:
            now()
        else:
            pl.when(cond)(now)
        books[-1][1].append((cond, slot, src.shape[0]))

    def deliver(cond, src, dst, rslot, til):
        send(both(cond, til != tile), src, dst, rslot, til)

        @pl.when(both(cond, til == tile))
        def _():
            dst[...] = src[...]
        _, slot, size = books[-1][1].pop()
        books[-1][1].append(((cond, til), slot, size))

    books = [(None, [])]

    def block(cond, body):
        books.append((cond, []))
        pl.when(cond)(body)
        books.append((None, []))

    def sent():
        def settle(entries):
            for cond, slot, size in entries:
                if isinstance(cond, tuple):
                    cond = both(cond[0], cond[1] != tile)
                ref = stand_in[size]

                def done():
                    remote(ref, ref, slot, 0, panel, tile).wait_send()
                if cond is None:
                    done()
                else:
                    pl.when(cond)(done)
        for cond, entries in books:
            if cond is None:
                settle(entries)
            else:
                pl.when(cond)(lambda: settle(entries))
        books[:] = [(None, [])]

    def arrived(cond, dst, rslot):
        def now():
            remote(dst, dst, 0, rslot, panel, tile).wait_recv()
        if cond is None:
            now()
        else:
            pl.when(cond)(now)

    def ends_in():
        for jj, piece, home, cond in end_homes:
            if 1 <= jj <= 16:
                deliver(yes, ext.at[pl.ds(8 * jj + 4 * piece, 4), 1], in_home.at[0, side, r],
                        IN_HOME + 2 * side + r, home)
    block(at_end, ends_in)
    for b, piece, home, cond in tile_homes:
        if b == 1:
            deliver(cond, tr.at[pl.ds(4 * piece, 4)], in_home.at[1, r, half],
                    IN_HOME + 4 + 2 * r + half, home)
    edge_src = ext.at[pl.ds(128 - 120 * r, 8), 1]
    send(None, edge_src, ext.at[pl.ds(136 * r, 8), 1], HALO, tid(other, c))
    send(has_right, edge_src, ext.at[pl.ds(136 * r, 8), 0], HALO + 1, tid(other, c + 1))
    send(has_left, edge_src, ext.at[pl.ds(136 * r, 8), 2], HALO + 2, tid(other, c - 1))
    mid = ext.at[pl.ds(8, 128), 1]
    send(has_right, mid, ext.at[pl.ds(8, 128), 0], HALO + 3, tid(r, c + 1))
    send(has_left, mid, ext.at[pl.ds(8, 128), 2], HALO + 4, tid(r, c - 1))

    def turned(landed, slot):
        pick, rev, flip = facts[slot]
        yf[...] = landed[pick].astype(F32).reshape(64, 128)
        turn = 1 - 2 * flip
        for high in range(2):
            for i in range(4):
                first = jnp.where(rev == 1, 32 * (1 - high) + 8 * (3 - i), 32 * high + 8 * i) + 7 * flip
                for d in range(8):
                    zf[pl.ds(32 * high + 8 * i + d, 1), :] = yf[pl.ds(first + turn * d, 1), :]
        return zf[0:64, :]

    def cross(landing, source, first_slot):
        def out_of_panel():
            for step in range(1, PANELS):
                send(None, source.at[step - 1], landing.at[3 - step], first_slot + 3 - step, tile,
                     lax.rem(panel + step, PANELS))
        block(is_home, out_of_panel)

    def hand_out(landing, first_slot):
        for i in range(3):
            remote(landing.at[i], landing.at[i], 0, first_slot + i, panel, tile).wait_recv()
        for slot in range(2):
            value = turned(landing, slot)
            blank = jnp.zeros_like(value)
            row_out[slot] = jnp.where(rowf, value, blank).astype(BF16).reshape(2, 4, 8, 128)
            col_out[slot] = jnp.where(rowf, blank, value).astype(BF16).reshape(2, 4, 8, 128)

    for k in range(0, CELLS, 64):
        some = jnp.broadcast_to(weight[pl.ds(k, 64)].reshape(1, 64), (128, 64))
        wrep[pl.ds(k, 64), :] = jnp.transpose(some, (1, 0))
    for n in range(NSUB):
        pltpu.make_async_copy(inv_hbm.at[n], inv.at[n], inv_sem.at[n]).wait()

    @pl.when(at_end)
    def _():
        place = lax.broadcasted_iota(jnp.int32, (CELLS, 192), 0)
        want = lax.broadcasted_iota(jnp.int32, (CELLS, 192), 1)
        want = 24 * lax.div(want, 8) + lax.rem(want, 8) + 16 * side
        choose = jnp.where(place == want, 1.0, 0.0).astype(BF16)

        def gather(n, carry):
            ends[n] = jnp.dot(inv[n], choose, preferred_element_type=F32).astype(BF16)
            return carry
        lax.fori_loop(0, NSUB, gather, 0)

    came_rows = []
    for slot in range(2):
        for high in range(2):
            k = (LAST - mu) if high else mu
            came_rows.append((1, slot, high, tid(slot, k)))
            came_rows.append((0, slot, high, tid(high, LAST * slot)))

    @pl.when(is_home)
    def _():
        for kind, slot, high, til in came_rows:
            arrived(til != tile, in_home.at[kind, slot, high], IN_HOME + 4 * kind + 2 * slot + high)
        for step in range(3):
            cross_out[step] = in_home[row_type, to_second[step]]
    cross(cross_in, cross_out, CROSS)

    spread[...] = jnp.zeros_like(spread)

    @pl.when(is_home)
    def _():
        hand_out(cross_in, CROSS)

    def ghosts_out():
        for slot, high, row, til, cond, at in served_ends:
            deliver(cond, col_out.at[slot, high], colg.at[pl.ds(at, 4)], COL_GHOST + at // 4, til)
        for slot, high, b, til, cond in served_rows:
            piece = (1 - part) if high else part
            deliver(cond, row_out.at[slot, high], rowg.at[pl.ds(8 * b + 4 * piece, 4)], ROW_GHOST + 2 * b + piece, til)
    block(is_home, ghosts_out)

    arrived(None, ext.at[pl.ds(inner_rows, 8), 1], HALO)
    arrived(has_left, ext.at[pl.ds(inner_rows, 8), 0], HALO + 1)
    arrived(has_right, ext.at[pl.ds(inner_rows, 8), 2], HALO + 2)
    arrived(has_left, ext.at[pl.ds(8, 128), 0], HALO + 3)
    arrived(has_right, ext.at[pl.ds(8, 128), 2], HALO + 4)
    flat = ext.reshape(144 * 24, 128)

    def solve(n, carry):
        rows = pl.ds(pl.multiple_of(n * 192, 64), CELLS)
        solved = jnp.dot(inv[n], flat[rows, :], preferred_element_type=F32)
        spread[rows, :] += solved * wrep[...]
        return carry

    lax.fori_loop(0, NSUB, solve, 0)

    end_cells = colg.reshape(144 * 8, 128)

    @pl.when(at_end)
    def _():
        for jj, piece, home, cond in end_homes:
            arrived(both(cond, home != tile), colg.at[pl.ds(8 * jj + 4 * piece, 4)], COL_GHOST + 2 * jj + piece)

        def add(n, carry):
            rows = pl.ds(pl.multiple_of(n * 192, 64), CELLS)
            some = end_cells[pl.ds(pl.multiple_of(n * 64, 64), 192), :]
            spread[rows, :] += jnp.dot(ends[n], some, preferred_element_type=F32) * wrep[...]
            return carry
        lax.fori_loop(0, NSUB, add, 0)

    for b, piece, home, cond in tile_homes:
        arrived(both(cond, home != tile), rowg.at[pl.ds(8 * b + 4 * piece, 4)], ROW_GHOST + 2 * b + piece)
    zf[...] = rowg[...].astype(F32).reshape(192, 128)
    for i in range(8):
        rg[24 * i:24 * i + 24, :] = zf[pl.ds(i, 24, stride=8), :]

    @pl.when(r == 0)
    def _():
        more = jnp.dot(inv[0][:, 0:192], rg[...].astype(BF16), preferred_element_type=F32)
        spread[0:CELLS, :] += more * wrep[...]

    @pl.when(r == 1)
    def _():
        more = jnp.dot(inv[NSUB - 1][:, 384:CELLS], rg[...].astype(BF16), preferred_element_type=F32)
        spread[192 * (NSUB - 1):, :] += more * wrep[...]

    cube = spread.reshape(144, 3, 8, 128)

    def ends_back():
        for i in range(0, 144, 16):
            colb[i:i + 16] = cube[i:i + 16, 2 * side].astype(BF16)
        for jj, piece, home, cond in end_homes:
            high = jnp.where(16 * r + jj - 1 >= 16, 1, 0)
            deliver(cond, colb.at[pl.ds(8 * jj + 4 * piece, 4)], col_back.at[side, high, r],
                    COL_BACK + 4 * side + 2 * high + r, home)
    block(at_end, ends_back)
    for p in range(24):
        rowt[p] = spread[pl.ds(24 * seam_rows + p, 8, stride=24), :].astype(BF16)
    for b, piece, home, cond in tile_homes:
        high = jnp.where(c + b - 1 >= 16, 1, 0)
        deliver(cond, rowt.at[pl.ds(8 * b + 4 * piece, 4)], row_back.at[r, high, b],
                ROW_BACK + 6 * r + 3 * high + b, home)
    for b in range(3):
        inners[b] = cube[pl.ds(inner_rows, 8), b].astype(BF16)
    send(None, inners.at[1], from_vert, HALO_BACK + 2, tid(other, c))
    send(has_left, inners.at[0], from_dr, HALO_BACK + 3, tid(other, c - 1))
    send(has_right, inners.at[2], from_dl, HALO_BACK + 4, tid(other, c + 1))
    for b in range(2):
        for i in range(0, 128, 16):
            sides[b, i:i + 16] = cube[8 + i:24 + i, 2 * b].astype(BF16)
    send(has_left, sides.at[0], from_right, HALO_BACK, tid(r, c - 1))
    send(has_right, sides.at[1], from_left, HALO_BACK + 1, tid(r, c + 1))

    @pl.when(is_home)
    def _():
        for slot, high, b, til, cond in served_rows:
            arrived(both(cond, til != tile), row_back.at[slot, high, b], ROW_BACK + 6 * slot + 3 * high + b)
        for slot, high, row, til, cond, _ in served_ends:
            arrived(both(cond, til != tile), col_back.at[slot, high, row], COL_BACK + 4 * slot + 2 * high + row)
        for slot in range(2):
            for high in range(2):
                by_row = row_back[slot, high, 0].astype(F32) + row_back[slot, high, 1].astype(F32)
                by_row = by_row + row_back[slot, high, 2].astype(F32)
                by_col = col_back[slot, high, 0].astype(F32) + col_back[slot, high, 1].astype(F32)
                mask = jnp.full((4, 8, 128), row_type, jnp.int32) == 1
                in_home[0, slot, high] = jnp.where(mask, by_row, by_col).astype(BF16)
        for step in range(3):
            back_out[step] = in_home[0, to_second[step]]
    cross(back_in, back_out, CROSS_BACK)

    arrived(has_right, from_right, HALO_BACK)
    arrived(has_left, from_left, HALO_BACK + 1)
    arrived(None, from_vert, HALO_BACK + 2)
    arrived(has_left, from_dl, HALO_BACK + 4)
    arrived(has_right, from_dr, HALO_BACK + 3)
    out[...] = cube[pl.ds(8, 128), 1]

    @pl.when(has_right)
    def _():
        out[...] += from_right[...].astype(F32)
        out[pl.ds(120 * other, 8)] += from_dr[...].astype(F32)

    @pl.when(has_left)
    def _():
        out[...] += from_left[...].astype(F32)
        out[pl.ds(120 * other, 8)] += from_dl[...].astype(F32)

    out[pl.ds(120 * other, 8)] += from_vert[...].astype(F32)

    sent()

    @pl.when(is_home)
    def _():
        hand_out(back_in, CROSS_BACK)

    def sums_out():
        for slot, high, row, til, cond, at in served_ends:
            if row == high:
                pos = highpos if high else lowpos
                deliver(yes, col_out.at[slot, high], corner_in.at[pl.ds(pos, 4)], COL_OWN + pos // 4, til)
        for slot, high, b, til, cond in served_rows:
            if b == 1:
                piece = (1 - part) if high else part
                deliver(yes, row_out.at[slot, high], own_back.at[pl.ds(4 * piece, 4)], ROW_OWN + piece, til)
    block(is_home, sums_out)
    for b, piece, home, cond in tile_homes:
        if b == 1:
            arrived(both(cond, home != tile), own_back.at[pl.ds(4 * piece, 4)], ROW_OWN + piece)
    xf[...] = own_back[...].astype(F32).reshape(64, 128)
    for i in range(8):
        out[120 * r + i] += xf[pl.ds(i, 8, stride=8), :]

    @pl.when(at_end)
    def _():
        for jj, piece, home, cond in end_homes:
            if 1 <= jj <= 16:
                arrived(home != tile, corner_in.at[pl.ds(8 * (jj - 1) + 4 * piece, 4)],
                        COL_OWN + 2 * (jj - 1) + piece)
        out[...] += corner_in[...].astype(F32)
    sent()


def local(residual, inverse, blend_weight, seam_table):
    def vmem(*shape, dtype=BF16):
        return pltpu.VMEM(shape, dtype)
    unit = (4, 8, 128)
    scratch = [
        vmem(NSUB, CELLS, CELLS),
        vmem(NSUB, CELLS, 192),
        vmem(CELLS, 128, dtype=F32),
        vmem(144, 3, 8, 128),
        vmem(144 * 24, 128, dtype=F32),
        vmem(144, 8, 128), vmem(144, 8, 128),
        vmem(2, H, 8, 128), vmem(3, 8, 8, 128),
        vmem(8, 8, 128),
        vmem(24, 8, 128),
        vmem(24, 8, 128),
        vmem(8, 8, 128),
        vmem(H, 8, 128),
        vmem(2, 2, 2, *unit),
        vmem(3, 2, *unit), vmem(3, 2, *unit),
        vmem(2, 2, *unit), vmem(2, 2, *unit),
        vmem(2, 2, 3, *unit),
        vmem(2, 2, 2, *unit),
        vmem(3, 2, *unit), vmem(3, 2, *unit),
        vmem(64, 128, dtype=F32),
        vmem(64, 128, dtype=F32),
        vmem(192, 128, dtype=F32),
        vmem(192, 128, dtype=F32),
        vmem(H, 8, 128), vmem(H, 8, 128),
        vmem(8, 8, 128), vmem(8, 8, 128), vmem(8, 8, 128),
        pltpu.SemaphoreType.DMA((NSUB,)),
        pltpu.SemaphoreType.DMA((SENDS,)),
        pltpu.SemaphoreType.DMA((RECVS,)),
    ]
    in_vmem = pl.BlockSpec(memory_space=pltpu.VMEM)
    out = pl.pallas_call(
        kernel,
        out_shape=jax.ShapeDtypeStruct((H, 8, 128), F32),
        in_specs=[pl.BlockSpec(memory_space=pltpu.SMEM), in_vmem, pl.BlockSpec(memory_space=pltpu.HBM), in_vmem],
        out_specs=in_vmem,
        scratch_shapes=scratch,
        compiler_params=pltpu.CompilerParams(
            collective_id=0, has_side_effects=True, vmem_limit_bytes=46 * 1024 * 1024),
        name="schwarz",
    )(jnp.transpose(seam_table, (2, 0, 1)), residual[0, 0], inverse[0, 0], blend_weight)
    return out[None, None]


def solution(mesh):
    placed = (P("panel", "tile", None, None, None), P("panel", "tile", None, None, None), P(), P())
    return jax.shard_map(
        local,
        mesh=mesh,
        in_specs=placed,
        out_specs=P("panel", "tile", None, None, None),
        check_vma=False,
    )
```

time: 63.8 us -> 56.9 us (0.89)
  the two profiles are of different devices: /device:TPU:17 before, /device:TPU:1 now
where the time goes in v2:
time: 56.9 us; the launch traced here: 56.7 us
  Pallas kernels  53.4 us (94%)
  local copies, waits for them, and re-layouts  3.21 us (6%)
    pallas_call x1, Pallas kernels, local(): pl.pallas_call(kernel, out_shape=jax.ShapeDtypeStruct((H, 8, 128), F32),...  53.4 us
    unnamed x7, local copies, waits for them, and re-layouts  3.21 us

profile of v2, /device:TPU:1, one launch (start us, length us, event | category | flops | bytes accessed | tf_op | source)
XLA Modules:
  0.0 56.7 jit_solution(17947441240730092219)
XLA Ops:
  0.0 0.0 copy-start
  0.0 1.0 %copy-done = f32[1,1,128,8,128]{4,3,2,1,0:T(8,128)S(1)} copy-done((f32[1,1,128,8,128]{4,3,2,1,0:T(8,128)S(1)}, f32[1,1,128,8,128]{4,3,2,1,0:T(8,128)}, u32[]{:S(2)}) %copy-start) | copy-done | bytes 524312
  1.0 0.0 copy-start.1
  1.0 0.7 %copy-done.1 = s32[4,4,3]{1,0,2:T(4,128)S(1)} copy-done((s32[4,4,3]{1,0,2:T(4,128)S(1)}, s32[4,4,3]{1,0,2:T(4,128)}, u32[]{:S(2)}) %copy-start.1) | copy-done | bytes 216
  1.7 0.0 copy-start.2
  1.7 0.7 %copy-done.2 = f32[576]{0:T(1024)S(1)} copy-done((f32[576]{0:T(1024)S(1)}, f32[576]{0:T(1024)}, u32[]{:S(2)}) %copy-start.2) | copy-done | bytes 2328
  2.4 53.4 %schwarz.1 = f32[128,8,128]{2,1,0:T(8,128)S(1)} custom-call(s32[3,4,4]{2,1,0:T(4,128)S(1)} %bitcast.6, f32[128,8,128]{2,1,0:T(8,128)S(1)} %bitcast.5, bf16[16,576,576]{2,1,0:T(8,128)(2,1)} %bitcast.7, f32[576]{0:T(1024)S(1)} %copy-done.2), custom_call_target="tpu_custom_call" | custom-call | tf_op jit(solution)/shard_map/schwarz/pallas_call | solution.py:540
  55.9 0.8 %copy.6 = f32[1,1,128,8,128]{4,3,2,1,0:T(8,128)} copy(f32[1,1,128,8,128]{4,3,2,1,0:T(8,128)S(1)} %bitcast.4) | data formatting | bytes 1048576
Async XLA Ops:
  0.0 1.0 %copy-start = (f32[1,1,128,8,128]{4,3,2,1,0:T(8,128)S(1)}, f32[1,1,128,8,128]{4,3,2,1,0:T(8,128)}, u32[]{:S(2)}) copy-start(f32[1,1,128,8,128]{4,3,2,1,0:T(8,128)} %param.4) | copy-start | bytes 1572868
  1.0 0.7 %copy-start.1 = (s32[4,4,3]{1,0,2:T(4,128)S(1)}, s32[4,4,3]{1,0,2:T(4,128)}, u32[]{:S(2)}) copy-start(s32[4,4,3]{1,0,2:T(4,128)} %param.7) | copy-start | bytes 580
  1.7 0.7 %copy-start.2 = (f32[576]{0:T(1024)S(1)}, f32[576]{0:T(1024)}, u32[]{:S(2)}) copy-start(f32[576]{0:T(1024)} %weight.1) | copy-start | bytes 6916

commit v3 on v2

--- a/solution.py
+++ b/solution.py
@@ -23,28 +23,19 @@
 RECVS = 120
 
 
-def home_of(mu, part):
-    z, x = mu % 8, mu // 8
-    low = min(z, 7 - z)
-    inner = low in (0, 3)
-    col = (1 if inner else 0) if z < 4 else (6 if inner else 7)
-    return (2 * (low // 2) + part) * 16 + (x ^ part) * 8 + (7 - col if part else col)
-
-
-def home_at(mu, part):
-    z, x = lax.rem(mu, 8), mu // 8
-    low = jnp.minimum(z, 7 - z)
-    inner = jnp.where(jnp.logical_or(low == 0, low == 3), 1, 0)
-    col = jnp.where(z < 4, inner, 7 - inner)
-    up = low // 2
-    if part:
-        return (2 * up + 1) * 16 + (1 - x) * 8 + 7 - col
-    return (2 * up) * 16 + x * 8 + col
-
-
-def kernel(seam, res, inv_hbm, weight, out, inv, ends, wrep, ext, spread, colg, colb, sides, inners, tr, rowg, rowt, own_back, corner_in,
+HOMES = ((7, 8), (41, 22), (9, 10), (2, 5), (26, 29), (14, 17), (15, 16), (39, 56),
+         (40, 55), (47, 33), (1, 30), (21, 34), (37, 42), (6, 25), (38, 48), (24, 23))
+
+
+def home_of(k, piece):
+    if k < 0 or k > LAST:
+        return -1
+    return HOMES[k][piece] if k < 16 else HOMES[LAST - k][1 - piece]
+
+
+def kernel(seam_hbm, res_hbm, inv_hbm, weight_hbm, out, seam, res, weight, inv, ends, wrep, ext, spread, colg, colb, sides, inners, tr, rowg, rowt, own_back, corner_in,
            in_home, cross_out, cross_in, row_out, col_out, row_back, col_back, back_out, back_in,
-           xf, yf, zf, rg, from_left, from_right, from_vert, from_dl, from_dr, inv_sem, send_sem, recv_sem):
+           xf, yf, zf, rg, from_left, from_right, from_vert, from_dl, from_dr, in_sem, inv_sem, send_sem, recv_sem):
     panel = lax.axis_index("panel")
     tile = lax.axis_index("tile")
     r = tile // TILE_COLS
@@ -59,33 +50,25 @@
     inner_rows = 136 * other
     yes = tile >= 0
 
-    ty, tx, tz = tile // 16, lax.rem(tile // 8, 2), lax.rem(tile, 8)
-    part = lax.rem(ty, 2)
-    z0 = jnp.where(part == 1, 7 - tz, tz)
-    is_home = jnp.logical_or(tz < 2, tz > 5)
-    inner = jnp.where(jnp.logical_or(tz == 1, tz == 6), 1, 0)
-    up = ty // 2
-    low = 2 * up + jnp.where(up == inner, 1, 0)
-    mu = 8 * jnp.where(part == 1, 1 - tx, tx) + jnp.where(z0 < 4, low, 7 - low)
+    role = jnp.int32(-1)
+    for m in range(16):
+        for p in range(2):
+            role = jnp.where(tile == HOMES[m][p], 2 * m + p, role)
+    is_home = role >= 0
+    role = jnp.maximum(role, 0)
+    mu, part = role // 2, lax.rem(role, 2)
     middle = mu == 15
 
     def tid(row, col):
         return row * TILE_COLS + col
 
-    def chunk_home(k, piece):
-        first = k < 16
-        m = jnp.where(first, k, LAST - k)
-        a, b = home_at(m, 0), home_at(m, 1)
-        return jnp.where(first, (a, b)[piece], (b, a)[piece])
-
     def end_home(j, piece):
-        def fixed(k):
-            if k < 0 or k > LAST:
-                return -1
-            m = k if k < 16 else LAST - k
-            return home_of(m, piece if k < 16 else 1 - piece)
-        return jnp.where(r == 0, fixed(j), fixed(16 + j))
-
+        return jnp.where(r == 0, home_of(j, piece), home_of(16 + j, piece))
+
+    inputs = [pltpu.make_async_copy(a, b, in_sem.at[i])
+              for i, (a, b) in enumerate(((res_hbm, res), (seam_hbm, seam), (weight_hbm, weight)))]
+    for copy in inputs:
+        copy.start()
     for n in range(NSUB):
         pltpu.make_async_copy(inv_hbm.at[n], inv.at[n], inv_sem.at[n]).start()
 
@@ -139,8 +122,10 @@
     tile_homes = []
     for b in range(3):
         for piece in range(2):
-            k = c + b - 1
-            tile_homes.append((b, piece, chunk_home(k, piece), within(k)))
+            home = jnp.int32(-1)
+            for i in range(TILE_COLS):
+                home = jnp.where(c == i, home_of(i + b - 1, piece), home)
+            tile_homes.append((b, piece, home, within(c + b - 1)))
     end_homes = []
     for jj in range(18):
         for piece in range(2):
@@ -177,6 +162,8 @@
         greeted[0] = greeted[0] + both(cond, home != tile).astype(jnp.int32)
     greeted[0] = greeted[0] + jnp.where(is_home, 3, 0)
 
+    for copy in inputs:
+        copy.wait()
     ext[8:136, 1] = res[...].astype(BF16)
     for b in range(3):
         ext[pl.ds(seam_rows, 8), b] = jnp.zeros((8, 8, 128), BF16)
@@ -508,6 +495,9 @@
         return pltpu.VMEM(shape, dtype)
     unit = (4, 8, 128)
     scratch = [
+        pltpu.SMEM((3, PANELS, 4), jnp.int32),
+        vmem(H, 8, 128, dtype=F32),
+        vmem(CELLS, dtype=F32),
         vmem(NSUB, CELLS, CELLS),
         vmem(NSUB, CELLS, 192),
         vmem(CELLS, 128, dtype=F32),
@@ -532,21 +522,22 @@
         vmem(192, 128, dtype=F32),
         vmem(H, 8, 128), vmem(H, 8, 128),
         vmem(8, 8, 128), vmem(8, 8, 128), vmem(8, 8, 128),
+        pltpu.SemaphoreType.DMA((3,)),
         pltpu.SemaphoreType.DMA((NSUB,)),
         pltpu.SemaphoreType.DMA((SENDS,)),
         pltpu.SemaphoreType.DMA((RECVS,)),
     ]
-    in_vmem = pl.BlockSpec(memory_space=pltpu.VMEM)
+    given = (jnp.transpose(seam_table, (2, 0, 1)), residual[0, 0], inverse[0, 0], blend_weight)
     out = pl.pallas_call(
         kernel,
         out_shape=jax.ShapeDtypeStruct((H, 8, 128), F32),
-        in_specs=[pl.BlockSpec(memory_space=pltpu.SMEM), in_vmem, pl.BlockSpec(memory_space=pltpu.HBM), in_vmem],
-        out_specs=in_vmem,
+        in_specs=[pl.BlockSpec(memory_space=pltpu.HBM)] * 4,
+        out_specs=pl.BlockSpec(memory_space=pltpu.VMEM),
         scratch_shapes=scratch,
         compiler_params=pltpu.CompilerParams(
             collective_id=0, has_side_effects=True, vmem_limit_bytes=46 * 1024 * 1024),
         name="schwarz",
-    )(jnp.transpose(seam_table, (2, 0, 1)), residual[0, 0], inverse[0, 0], blend_weight)
+    )(*[pltpu.with_memory_space_constraint(a, pltpu.HBM) for a in given])
     return out[None, None]
 
 

time: 56.9 us -> 52.9 us (0.930)
  local copies, waits for them, and re-layouts: 3.21 us -> 0.8 us
  Pallas kernels: 53.4 us -> 52 us
    unnamed x7 -> x1, local copies, waits for them, and re-layouts: 3.21 us -> 0.8 us
    pallas_call x1, Pallas kernels: 53.4 us -> 52 us  [local(): pl.pallas_call(kernel, out_shape=jax.ShapeDtypeStruct((H, 8, 128), F32),...]
where the time goes in v3:
time: 52.9 us
  Pallas kernels  52 us (98%)
  local copies, waits for them, and re-layouts  0.8 us (2%)
    pallas_call x1, Pallas kernels, local(): pl.pallas_call(kernel, out_shape=jax.ShapeDtypeStruct((H, 8, 128), F32),...  52 us

profile of v3, /device:TPU:1, one launch (start us, length us, event | category | flops | bytes accessed | tf_op | source)
XLA Modules:
  0.0 52.9 jit_solution(5325072991202935826)
XLA Ops:
  0.0 52.0 %schwarz.1 = f32[128,8,128]{2,1,0:T(8,128)S(1)} custom-call(s32[3,4,4]{2,1,0:T(4,128)} %bitcast.7, f32[128,8,128]{2,1,0:T(8,128)} %bitcast.6, bf16[16,576,576]{2,1,0:T(8,128)(2,1)} %bitcast.5, f32[576]{0:T(1024)} %weight_hbm.1), custom_call_target="tpu_custom_call" | custom-call | tf_op jit(solution)/shard_map/schwarz/pallas_call | solution.py:531
  52.1 0.8 %copy.6 = f32[1,1,128,8,128]{4,3,2,1,0:T(8,128)} copy(f32[1,1,128,8,128]{4,3,2,1,0:T(8,128)S(1)} %bitcast.4) | data formatting | bytes 1048576

commit v4 on v3

--- a/solution.py
+++ b/solution.py
@@ -12,7 +12,8 @@
 NSUB = 16
 CELLS = 576
 MESH = pl.DeviceIdType.MESH
-SENDS = 130
+SENDS = 140
+FIRST = 7
 BF16, F32 = jnp.bfloat16, jnp.float32
 
 HALO, HALO_BACK = 0, 5
@@ -20,7 +21,9 @@
 ROW_GHOST, COL_GHOST = 24, 30
 ROW_BACK, COL_BACK = 66, 78
 ROW_OWN, COL_OWN = 86, 88
-RECVS = 120
+LATE_ROWS = 120
+HALO_REST = 122
+RECVS = 124
 
 
 HOMES = ((7, 8), (41, 22), (9, 10), (2, 5), (26, 29), (14, 17), (15, 16), (39, 56),
@@ -33,7 +36,7 @@
     return HOMES[k][piece] if k < 16 else HOMES[LAST - k][1 - piece]
 
 
-def kernel(seam_hbm, res_hbm, inv_hbm, weight_hbm, out, seam, res, weight, inv, ends, wrep, ext, spread, colg, colb, sides, inners, tr, rowg, rowt, own_back, corner_in,
+def kernel(seam_hbm, res_hbm, inv_hbm, weight_hbm, out, seam, res, weight, inv, ends, facing_ends, wide, colsum, wrep, ext, spread, colg, colb, sides, inners, tr, rowg, rowt, own_back, corner_in,
            in_home, cross_out, cross_in, row_out, col_out, row_back, col_back, back_out, back_in,
            xf, yf, zf, rg, from_left, from_right, from_vert, from_dl, from_dr, in_sem, inv_sem, send_sem, recv_sem):
     panel = lax.axis_index("panel")
@@ -198,7 +201,7 @@
             device_id=(pan, til), device_id_type=MESH)
 
     used = [0]
-    stand_in = {4: tr.at[pl.ds(0, 4)], 8: tr, 128: corner_in, 2: cross_out.at[0]}
+    stand_in = {64: corner_in.at[pl.ds(0, 64)], 16: corner_in.at[pl.ds(0, 16)], 112: corner_in.at[pl.ds(0, 112)], 4: tr.at[pl.ds(0, 4)], 8: tr, 128: corner_in, 2: cross_out.at[0]}
 
     def send(cond, src, dst, rslot, til, pan=None):
         pan = panel if pan is None else pan
@@ -271,9 +274,9 @@
     send(None, edge_src, ext.at[pl.ds(136 * r, 8), 1], HALO, tid(other, c))
     send(has_right, edge_src, ext.at[pl.ds(136 * r, 8), 0], HALO + 1, tid(other, c + 1))
     send(has_left, edge_src, ext.at[pl.ds(136 * r, 8), 2], HALO + 2, tid(other, c - 1))
-    mid = ext.at[pl.ds(8, 128), 1]
-    send(has_right, mid, ext.at[pl.ds(8, 128), 0], HALO + 3, tid(r, c + 1))
-    send(has_left, mid, ext.at[pl.ds(8, 128), 2], HALO + 4, tid(r, c - 1))
+    for piece, first in ((pl.ds(8, 64), HALO + 3), (pl.ds(72, 64), HALO_REST)):
+        send(has_right, ext.at[piece, 1], ext.at[piece, 0], first, tid(r, c + 1))
+        send(has_left, ext.at[piece, 1], ext.at[piece, 2], first + 1, tid(r, c - 1))
 
     def turned(landed, slot):
         pick, rev, flip = facts[slot]
@@ -315,8 +318,13 @@
         want = 24 * lax.div(want, 8) + lax.rem(want, 8) + 16 * side
         choose = jnp.where(place == want, 1.0, 0.0).astype(BF16)
 
+        by_block = wide.reshape(24, 3, 8, 192)
+
         def gather(n, carry):
-            ends[n] = jnp.dot(inv[n], choose, preferred_element_type=F32).astype(BF16)
+            found = jnp.dot(inv[n], choose, preferred_element_type=F32)
+            ends[n] = found.astype(BF16)
+            wide[...] = found
+            facing_ends[n] = by_block[:, 2 * side].reshape(192, 192).astype(BF16)
             return carry
         lax.fori_loop(0, NSUB, gather, 0)
 
@@ -336,6 +344,21 @@
     cross(cross_in, cross_out, CROSS)
 
     spread[...] = jnp.zeros_like(spread)
+
+    arrived(None, ext.at[pl.ds(inner_rows, 8), 1], HALO)
+    arrived(has_left, ext.at[pl.ds(inner_rows, 8), 0], HALO + 1)
+    arrived(has_right, ext.at[pl.ds(inner_rows, 8), 2], HALO + 2)
+    arrived(has_left, ext.at[pl.ds(8, 64), 0], HALO + 3)
+    arrived(has_right, ext.at[pl.ds(8, 64), 2], HALO + 4)
+    flat = ext.reshape(144 * 24, 128)
+
+    def solve(n, carry):
+        rows = pl.ds(pl.multiple_of(n * 192, 64), CELLS)
+        solved = jnp.dot(inv[n], flat[rows, :], preferred_element_type=F32)
+        spread[rows, :] += solved * wrep[...]
+        return carry
+
+    lax.fori_loop(0, FIRST, solve, 0, unroll=True)
 
     @pl.when(is_home)
     def _():
@@ -349,20 +372,24 @@
             deliver(cond, row_out.at[slot, high], rowg.at[pl.ds(8 * b + 4 * piece, 4)], ROW_GHOST + 2 * b + piece, til)
     block(is_home, ghosts_out)
 
-    arrived(None, ext.at[pl.ds(inner_rows, 8), 1], HALO)
-    arrived(has_left, ext.at[pl.ds(inner_rows, 8), 0], HALO + 1)
-    arrived(has_right, ext.at[pl.ds(inner_rows, 8), 2], HALO + 2)
-    arrived(has_left, ext.at[pl.ds(8, 128), 0], HALO + 3)
-    arrived(has_right, ext.at[pl.ds(8, 128), 2], HALO + 4)
-    flat = ext.reshape(144 * 24, 128)
-
-    def solve(n, carry):
-        rows = pl.ds(pl.multiple_of(n * 192, 64), CELLS)
-        solved = jnp.dot(inv[n], flat[rows, :], preferred_element_type=F32)
-        spread[rows, :] += solved * wrep[...]
-        return carry
-
-    lax.fori_loop(0, NSUB, solve, 0)
+    arrived(has_left, ext.at[pl.ds(72, 64), 0], HALO_REST)
+    arrived(has_right, ext.at[pl.ds(72, 64), 2], HALO_REST + 1)
+    lax.fori_loop(FIRST, NSUB, solve, 0, unroll=3)
+
+    cube = spread.reshape(144, 3, 8, 128)
+    clear = pl.ds(16 * other, 112)
+    not_end = jnp.logical_not(at_end)
+
+    def clear_rows():
+        for b in range(2):
+            for i in range(0, 112, 16):
+                sides[b, pl.ds(16 * other + i, 16)] = cube[pl.ds(8 + 16 * other + i, 16), 2 * b].astype(BF16)
+
+    @pl.when(not_end)
+    def _():
+        clear_rows()
+    send(not_end, sides.at[0, clear], from_right.at[clear], HALO_BACK, tid(r, c - 1))
+    send(not_end, sides.at[1, clear], from_left.at[clear], HALO_BACK + 1, tid(r, c + 1))
 
     end_cells = colg.reshape(144 * 8, 128)
 
@@ -371,6 +398,53 @@
         for jj, piece, home, cond in end_homes:
             arrived(both(cond, home != tile), colg.at[pl.ds(8 * jj + 4 * piece, 4)], COL_GHOST + 2 * jj + piece)
 
+
+    for b, piece, home, cond in tile_homes:
+        arrived(both(cond, home != tile), rowg.at[pl.ds(8 * b + 4 * piece, 4)], ROW_GHOST + 2 * b + piece)
+    zf[...] = rowg[...].astype(F32).reshape(192, 128)
+    for i in range(8):
+        rg[24 * i:24 * i + 24, :] = zf[pl.ds(i, 24, stride=8), :]
+
+    @pl.when(r == 0)
+    def _():
+        more = jnp.dot(inv[0][:, 0:192], rg[...].astype(BF16), preferred_element_type=F32)
+        spread[0:CELLS, :] += more * wrep[...]
+
+    @pl.when(r == 1)
+    def _():
+        more = jnp.dot(inv[NSUB - 1][:, 384:CELLS], rg[...].astype(BF16), preferred_element_type=F32)
+        spread[192 * (NSUB - 1):, :] += more * wrep[...]
+
+    @pl.when(at_end)
+    def _():
+        edge_weight = wrep.reshape(24, 3, 8, 128)[:, 2 * side].reshape(192, 128)
+        for i in range(0, 144, 16):
+            colsum[8 * i:8 * i + 128, :] = cube[i:i + 16, 2 * side].reshape(128, 128)
+
+        def add_first(n, carry):
+            rows = pl.ds(pl.multiple_of(n * 64, 64), 192)
+            colsum[rows, :] += jnp.dot(facing_ends[n], end_cells[rows, :], preferred_element_type=F32) * edge_weight
+            return carry
+        lax.fori_loop(0, NSUB, add_first, 0)
+
+    def ends_back():
+        for i in range(0, 144, 16):
+            colb[i:i + 16] = colsum[8 * i:8 * i + 128, :].reshape(16, 8, 128).astype(BF16)
+        for jj, piece, home, cond in end_homes:
+            high = jnp.where(16 * r + jj - 1 >= 16, 1, 0)
+            deliver(cond, colb.at[pl.ds(8 * jj + 4 * piece, 4)], col_back.at[side, high, r],
+                    COL_BACK + 4 * side + 2 * high + r, home)
+    block(at_end, ends_back)
+
+    for p in range(24):
+        rowt[p] = spread[pl.ds(24 * seam_rows + p, 8, stride=24), :].astype(BF16)
+    for b, piece, home, cond in tile_homes:
+        high = jnp.where(c + b - 1 >= 16, 1, 0)
+        deliver(cond, rowt.at[pl.ds(8 * b + 4 * piece, 4)], row_back.at[r, high, b],
+                ROW_BACK + 6 * r + 3 * high + b, home)
+
+    @pl.when(at_end)
+    def _():
         def add(n, carry):
             rows = pl.ds(pl.multiple_of(n * 192, 64), CELLS)
             some = end_cells[pl.ds(pl.multiple_of(n * 64, 64), 192), :]
@@ -378,48 +452,22 @@
             return carry
         lax.fori_loop(0, NSUB, add, 0)
 
-    for b, piece, home, cond in tile_homes:
-        arrived(both(cond, home != tile), rowg.at[pl.ds(8 * b + 4 * piece, 4)], ROW_GHOST + 2 * b + piece)
-    zf[...] = rowg[...].astype(F32).reshape(192, 128)
-    for i in range(8):
-        rg[24 * i:24 * i + 24, :] = zf[pl.ds(i, 24, stride=8), :]
-
-    @pl.when(r == 0)
-    def _():
-        more = jnp.dot(inv[0][:, 0:192], rg[...].astype(BF16), preferred_element_type=F32)
-        spread[0:CELLS, :] += more * wrep[...]
-
-    @pl.when(r == 1)
-    def _():
-        more = jnp.dot(inv[NSUB - 1][:, 384:CELLS], rg[...].astype(BF16), preferred_element_type=F32)
-        spread[192 * (NSUB - 1):, :] += more * wrep[...]
-
-    cube = spread.reshape(144, 3, 8, 128)
-
-    def ends_back():
-        for i in range(0, 144, 16):
-            colb[i:i + 16] = cube[i:i + 16, 2 * side].astype(BF16)
-        for jj, piece, home, cond in end_homes:
-            high = jnp.where(16 * r + jj - 1 >= 16, 1, 0)
-            deliver(cond, colb.at[pl.ds(8 * jj + 4 * piece, 4)], col_back.at[side, high, r],
-                    COL_BACK + 4 * side + 2 * high + r, home)
-    block(at_end, ends_back)
-    for p in range(24):
-        rowt[p] = spread[pl.ds(24 * seam_rows + p, 8, stride=24), :].astype(BF16)
-    for b, piece, home, cond in tile_homes:
-        high = jnp.where(c + b - 1 >= 16, 1, 0)
-        deliver(cond, rowt.at[pl.ds(8 * b + 4 * piece, 4)], row_back.at[r, high, b],
-                ROW_BACK + 6 * r + 3 * high + b, home)
     for b in range(3):
         inners[b] = cube[pl.ds(inner_rows, 8), b].astype(BF16)
     send(None, inners.at[1], from_vert, HALO_BACK + 2, tid(other, c))
     send(has_left, inners.at[0], from_dr, HALO_BACK + 3, tid(other, c - 1))
     send(has_right, inners.at[2], from_dl, HALO_BACK + 4, tid(other, c + 1))
     for b in range(2):
-        for i in range(0, 128, 16):
-            sides[b, i:i + 16] = cube[8 + i:24 + i, 2 * b].astype(BF16)
-    send(has_left, sides.at[0], from_right, HALO_BACK, tid(r, c - 1))
-    send(has_right, sides.at[1], from_left, HALO_BACK + 1, tid(r, c + 1))
+        sides[b, pl.ds(112 * r, 16)] = cube[pl.ds(8 + 112 * r, 16), 2 * b].astype(BF16)
+    late = pl.ds(112 * r, 16)
+    send(has_left, sides.at[0, late], from_right.at[late], LATE_ROWS, tid(r, c - 1))
+    send(has_right, sides.at[1, late], from_left.at[late], LATE_ROWS + 1, tid(r, c + 1))
+
+    @pl.when(at_end)
+    def _():
+        clear_rows()
+    send(both(at_end, has_left), sides.at[0, clear], from_right.at[clear], HALO_BACK, tid(r, c - 1))
+    send(both(at_end, has_right), sides.at[1, clear], from_left.at[clear], HALO_BACK + 1, tid(r, c + 1))
 
     @pl.when(is_home)
     def _():
@@ -438,25 +486,6 @@
             back_out[step] = in_home[0, to_second[step]]
     cross(back_in, back_out, CROSS_BACK)
 
-    arrived(has_right, from_right, HALO_BACK)
-    arrived(has_left, from_left, HALO_BACK + 1)
-    arrived(None, from_vert, HALO_BACK + 2)
-    arrived(has_left, from_dl, HALO_BACK + 4)
-    arrived(has_right, from_dr, HALO_BACK + 3)
-    out[...] = cube[pl.ds(8, 128), 1]
-
-    @pl.when(has_right)
-    def _():
-        out[...] += from_right[...].astype(F32)
-        out[pl.ds(120 * other, 8)] += from_dr[...].astype(F32)
-
-    @pl.when(has_left)
-    def _():
-        out[...] += from_left[...].astype(F32)
-        out[pl.ds(120 * other, 8)] += from_dl[...].astype(F32)
-
-    out[pl.ds(120 * other, 8)] += from_vert[...].astype(F32)
-
     sent()
 
     @pl.when(is_home)
@@ -473,6 +502,27 @@
                 piece = (1 - part) if high else part
                 deliver(yes, row_out.at[slot, high], own_back.at[pl.ds(4 * piece, 4)], ROW_OWN + piece, til)
     block(is_home, sums_out)
+    arrived(has_right, from_right.at[clear], HALO_BACK)
+    arrived(has_left, from_left.at[clear], HALO_BACK + 1)
+    arrived(has_right, from_right.at[late], LATE_ROWS)
+    arrived(has_left, from_left.at[late], LATE_ROWS + 1)
+    arrived(None, from_vert, HALO_BACK + 2)
+    arrived(has_left, from_dl, HALO_BACK + 4)
+    arrived(has_right, from_dr, HALO_BACK + 3)
+    out[...] = cube[pl.ds(8, 128), 1]
+
+    @pl.when(has_right)
+    def _():
+        out[...] += from_right[...].astype(F32)
+        out[pl.ds(120 * other, 8)] += from_dr[...].astype(F32)
+
+    @pl.when(has_left)
+    def _():
+        out[...] += from_left[...].astype(F32)
+        out[pl.ds(120 * other, 8)] += from_dl[...].astype(F32)
+
+    out[pl.ds(120 * other, 8)] += from_vert[...].astype(F32)
+
     for b, piece, home, cond in tile_homes:
         if b == 1:
             arrived(both(cond, home != tile), own_back.at[pl.ds(4 * piece, 4)], ROW_OWN + piece)
@@ -500,6 +550,9 @@
         vmem(CELLS, dtype=F32),
         vmem(NSUB, CELLS, CELLS),
         vmem(NSUB, CELLS, 192),
+        vmem(NSUB, 192, 192),
+        vmem(CELLS, 192, dtype=F32),
+        vmem(144 * 8, 128, dtype=F32),
         vmem(CELLS, 128, dtype=F32),
         vmem(144, 3, 8, 128),
         vmem(144 * 24, 128, dtype=F32),

time: 52.9 us -> 50.8 us (0.960)
  Pallas kernels: 52 us -> 49.9 us
    pallas_call x1, Pallas kernels: 52 us -> 49.9 us  [local(): pl.pallas_call(kernel, out_shape=jax.ShapeDtypeStruct((H, 8, 128), F32),...]
where the time goes in v4:
time: 50.8 us; the launch traced here: 50.7 us
  Pallas kernels  49.9 us (98%)
  local copies, waits for them, and re-layouts  0.8 us (2%)
    pallas_call x1, Pallas kernels, local(): pl.pallas_call(kernel, out_shape=jax.ShapeDtypeStruct((H, 8, 128), F32),...  49.9 us

profile of v4, /device:TPU:1, one launch (start us, length us, event | category | flops | bytes accessed | tf_op | source)
XLA Modules:
  0.0 50.7 jit_solution(2358083009840172000)
XLA Ops:
  0.0 49.9 %schwarz.1 = f32[128,8,128]{2,1,0:T(8,128)S(1)} custom-call(s32[3,4,4]{2,1,0:T(4,128)} %bitcast.7, f32[128,8,128]{2,1,0:T(8,128)} %bitcast.6, bf16[16,576,576]{2,1,0:T(8,128)(2,1)} %bitcast.5, f32[576]{0:T(1024)} %weight_hbm.1), custom_call_target="tpu_custom_call" | custom-call | tf_op jit(solution)/shard_map/schwarz/pallas_call | solution.py:584
  49.9 0.8 %copy.6 = f32[1,1,128,8,128]{4,3,2,1,0:T(8,128)} copy(f32[1,1,128,8,128]{4,3,2,1,0:T(8,128)S(1)} %bitcast.4) | data formatting | bytes 1048576
